TPU v7x, 32 devices: a whole 2x2x4 slice. The times are simulated.
32 devices in a mesh: row: 4 (over y, x), col: 8 (over z, core).
Axes of the slice: x: 2, y: 2, z: 4, core: 2. Of those that a mesh axis runs over, the one named last changes fastest.
Arguments:
- patches: bfloat16 [32, 128, 768], P('row', 'col'), may hold values from -6 to 6
- w_patch: bfloat16 [768, 6144], replicated, may hold values from -0.21875 to 0.21875
- patch_bias: bfloat16 [6144], replicated, may hold values from -5 to 5
- ln_gain: bfloat16 [6144], replicated, may hold values from 0.5 to 1.5
- w_qkv: bfloat16 [6144, 3, 48, 128], P(None, None, 'col'), may hold values from -1 to 1
- qk_gain: float32 [2, 48, 128], P(None, 'col'), may hold values from 0 to 6, as said below
- w_out: bfloat16 [48, 128, 6144], P('col', None, 'row'), may hold values from -0.078125 to 0.078125
Outputs:
- attn_branch: bfloat16 [4096, 6144], P(('row', 'col'))
Inputs may be any that keep to these rules, and one draw needn't show every extreme that they name: `qk_gain`: positive gains.
All inputs are finite; a program needn't handle non-finite values.
Results may differ from a plain program's by a relative error of at most 0.015.
Values may be sent and summed in bfloat16 or wider, within the bound.
A program may use at most 320 MiB of HBM per device.

v0:
```python
import functools
import math

import jax
import jax.numpy as jnp
from jax import lax
from jax.experimental import pallas as pl
from jax.experimental.pallas import tpu as pltpu
from jax.sharding import PartitionSpec as P

NORM_EPS = 1e-06
KEY_BLOCK = 1024
CHUNKS = 4


def sincos_half(ids, model_width):
    quarter = model_width // 4
    frequency = 1.0 / 10000.0 ** (jnp.arange(quarter, dtype=jnp.float32) / quarter)
    angle = ids.astype(jnp.float32)[:, None] * frequency[None, :]
    return jnp.concatenate([jnp.sin(angle), jnp.cos(angle)], axis=1)


def layer_norm(values, gain_row):
    mean_val = jnp.mean(values, axis=-1, keepdims=True)
    centered = values - mean_val
    variance = jnp.mean(centered * centered, axis=-1, keepdims=True)
    return centered * lax.rsqrt(variance + NORM_EPS) * gain_row


def attention_kernel(key_block, exp_factor, q_ref, k_ref, v_ref, out_ref):
    rows, head_size = math.prod(q_ref.shape[:-1]), q_ref.shape[-1]
    query = q_ref[...].reshape(rows, head_size)
    peak = jnp.full((rows, 1), -1e30, jnp.float32)
    total = jnp.zeros((rows, 1), jnp.float32)
    acc = jnp.zeros((rows, head_size), jnp.float32)
    for start in range(0, k_ref.shape[0], key_block):
        scores = lax.dot_general(
            query,
            k_ref[start : start + key_block, :],
            (((1,), (1,)), ((), ())),
            preferred_element_type=jnp.float32,
        )
        new_peak = jnp.maximum(peak, jnp.max(scores, axis=1, keepdims=True) * exp_factor)
        rescale = jnp.exp2(peak - new_peak)
        weights = jnp.exp2(scores * exp_factor - new_peak)
        total = total * rescale + jnp.sum(weights, axis=1, keepdims=True)
        acc = acc * rescale + jnp.dot(
            weights.astype(jnp.bfloat16),
            v_ref[start : start + key_block, :],
            preferred_element_type=jnp.float32,
        )
        peak = new_peak
    out_ref[...] = (acc / total).astype(out_ref.dtype).reshape(out_ref.shape)


def attention(queries, keys_values, chunk, chunk_rows, width, head_size):
    owners = queries.shape[0]
    heads = width // head_size
    key_count = keys_values.shape[0]
    key_block = math.gcd(key_count, KEY_BLOCK)
    exp_factor = math.log2(math.e) / math.sqrt(head_size)
    rows = owners * chunk_rows
    elements = heads * rows * key_count
    return pl.pallas_call(
        functools.partial(attention_kernel, key_block, exp_factor),
        grid=(heads,),
        in_specs=[
            pl.BlockSpec((owners, chunk_rows, head_size), lambda h: (0, chunk, h)),
            pl.BlockSpec((key_count, head_size), lambda h: (0, h)),
            pl.BlockSpec((key_count, head_size), lambda h: (0, heads + h)),
        ],
        out_specs=pl.BlockSpec((owners, chunk_rows, head_size), lambda h: (0, 0, h)),
        out_shape=jax.ShapeDtypeStruct((owners, chunk_rows, width), jnp.bfloat16),
        compiler_params=pltpu.CompilerParams(
            dimension_semantics=("arbitrary",),
            vmem_limit_bytes=48 * 1024 * 1024,
        ),
        cost_estimate=pl.CostEstimate(
            flops=4 * elements * head_size,
            bytes_accessed=4 * (rows + key_count) * width,
            transcendentals=elements,
        ),
        name="attention",
    )(queries, keys_values, keys_values)


def norm_kernel(x_ref, gain_ref, out_ref):
    out_ref[...] = layer_norm(x_ref[...], gain_ref[...]).astype(out_ref.dtype)


def norm_heads(projected, gain_row, head_size):
    rows, width = projected.shape[0], gain_row.shape[1]
    return pl.pallas_call(
        norm_kernel,
        grid=(width // head_size,),
        in_specs=[
            pl.BlockSpec((rows, head_size), lambda h: (0, h)),
            pl.BlockSpec((1, head_size), lambda h: (0, h)),
        ],
        out_specs=pl.BlockSpec((rows, head_size), lambda h: (0, h)),
        out_shape=jax.ShapeDtypeStruct((rows, width), jnp.bfloat16),
        compiler_params=pltpu.CompilerParams(dimension_semantics=("arbitrary",)),
        cost_estimate=pl.CostEstimate(
            flops=10 * rows * width, bytes_accessed=6 * rows * width, transcendentals=rows
        ),
        name="norm_heads",
    )(projected, gain_row)


def local(patches, w_patch, patch_bias, ln_gain, w_qkv, qk_gain, w_out):
    tile_rows, tile_cols, pixel_width = patches.shape
    model_width = w_patch.shape[1]
    heads_here = w_qkv.shape[2]
    head_size = w_qkv.shape[3]
    col_count = lax.axis_size("col")
    block_tokens = tile_rows * tile_cols * col_count
    row_anchor = lax.axis_index("row") * tile_rows
    qkv_matrix = w_qkv.reshape(model_width, 3 * heads_here * head_size)
    bias_row = patch_bias.astype(jnp.float32)[None, :]
    gain_row = ln_gain.astype(jnp.float32)
    pixels = lax.all_gather(patches, "col", axis=1, tiled=True)
    piece_cols = pixels.shape[1]
    flat_pixels = pixels.reshape(tile_rows * piece_cols, pixel_width)
    embedded = jnp.dot(flat_pixels, w_patch, preferred_element_type=jnp.float32) + bias_row
    row_half = sincos_half(row_anchor + jnp.arange(tile_rows, dtype=jnp.int32), model_width)
    col_half = sincos_half(jnp.arange(piece_cols, dtype=jnp.int32), model_width)
    row_half, col_half = lax.optimization_barrier((row_half, col_half))
    half_shape = (tile_rows, piece_cols, model_width // 2)
    position = jnp.concatenate(
        [
            jnp.broadcast_to(row_half[:, None, :], half_shape),
            jnp.broadcast_to(col_half[None, :, :], half_shape),
        ],
        axis=2,
    )
    embedded = embedded + position.reshape(tile_rows * piece_cols, model_width)
    normed = layer_norm(embedded, gain_row).astype(jnp.bfloat16)
    normed_piece = normed.reshape(tile_rows, piece_cols, model_width)
    project_piece_cols = normed_piece.shape[1]
    flat_normed = normed_piece.reshape(tile_rows * project_piece_cols, model_width)
    projected = jnp.dot(flat_normed, qkv_matrix, preferred_element_type=jnp.float32)
    head_width = heads_here * head_size
    gain_qk = qk_gain.reshape(1, 2 * head_width)
    normed_qk = norm_heads(projected, gain_qk, head_size)
    keys_values = jnp.concatenate(
        [normed_qk[:, head_width:], projected[:, 2 * head_width :].astype(jnp.bfloat16)], axis=1
    )
    keys_values = lax.all_gather(keys_values, "row", axis=0, tiled=True)
    out_weight = lax.all_gather(w_out, "row", axis=2, tiled=True).reshape(
        heads_here * head_size, model_width
    )
    owned = block_tokens // col_count
    chunk_rows = owned // math.gcd(owned // 16, CHUNKS)
    queries = normed_qk.reshape(col_count, owned, 2 * head_width)
    pieces = []
    for chunk in range(owned // chunk_rows):
        context = attention(queries, keys_values, chunk, chunk_rows, head_width, head_size)
        partial = jnp.dot(
            context.reshape(col_count * chunk_rows, head_width),
            out_weight,
            preferred_element_type=jnp.float32,
        ).astype(jnp.bfloat16)
        pieces.append(lax.psum_scatter(partial, "col", scatter_dimension=0, tiled=True))
    return jnp.concatenate(pieces, axis=0)


def solution(mesh):
    return jax.shard_map(
        local,
        mesh=mesh,
        in_specs=(
            P("row", "col", None),
            P(),
            P(),
            P(),
            P(None, None, "col", None),
            P(None, "col", None),
            P("col", None, "row"),
        ),
        out_specs=P(("row", "col"), None),
        check_vma=False,
    )
```

profile of v0, /device:TPU:0, one launch (start us, length us, event | category | flops | bytes accessed | tf_op | source)
XLA Modules:
  0.0 561.8 jit_solution(9421970326799950756)
XLA Ops:
  7.6 2.8 multiply_sine_fusion
  11.2 37.0 %copy.9 = bf16[6144,3,6,128]{0,3,2,1:T(8,128)(2,1)} copy(bf16[6144,3,6,128]{3,0,2,1:T(8,128)(2,1)} %param.11) | data formatting | bytes 56623104 | tf_op args[4]
  52.0 11.2 %pad_maximum_fusion = f32[8,128,6144]{2,1,0:T(8,128)} fusion(f32[8,128,3072]{2,1,0:T(8,128)S(1)} %broadcast_in_dim.5, f32[8,128,3072]{2,1,0:T(8,128)S(1)} %broadcast_in_dim.4), kind=kLoop, calls=%fused_computation | loop fusion | flops 6291456 | bytes 50331648 | tf_op jit(solution)/shard_map/concatenate | solution.py:129
  63.2 25.3 %fusion.4 = (f32[1024]{0:T(1024)S(1)}, f32[1024,6144]{1,0:T(8,128)}) fusion(f32[8,128,6144]{2,1,0:T(8,128)} %pad_maximum_fusion, f32[6144]{0:T(1024)S(1)} %convert_element_type.38, bf16[1024,768]{1,0:T(8,128)(2,1)} %bitcast.34, bf16[768,6144]{1,0:T(8,128)(2,1)} %param.8), kind=kOutput, calls=%fused_computation.26 | convolution fusion | flops 9682549760 | bytes 61370368 | tf_op jit(solution)/shard_map/dot_general | solution.py:124
  88.5 10.2 %multiply_reduce_fusion = f32[1024]{0:T(1024)S(1)} fusion(f32[1024,6144]{1,0:T(8,128)} %get-tuple-element.14, f32[1024]{0:T(1024)S(1)} %broadcast_multiply_fusion), kind=kLoop, calls=%fused_computation.3 | loop fusion | flops 18873344 | bytes 25174016 | tf_op jit(solution)/shard_map/reduce_sum | solution.py:26
  98.7 39.0 %fusion.x_ref = f32[1024,2304]{1,0:T(8,128)} fusion(bf16[6144,2304]{0,1:T(8,128)(2,1)} %bitcast.29, f32[1024,6144]{1,0:T(8,128)} %get-tuple-element.14, f32[6144]{0:T(1024)S(1)} %convert_element_type.41, f32[1024]{0:T(1024)S(1)} %add_rsqrt_fusion, f32[1024]{0:T(1024)S(1)} %broadcast_multiply_fusion), kind=kOutput, calls=%fused_computation.4 | convolution fusion | flops 29016195072 | bytes 62947328 | tf_op jit(solution)/shard_map/dot_general | solution.py:141
  137.7 3.2 slice.12
  140.9 10.5 %norm_heads.1 = bf16[1024,1536]{1,0:T(8,128)(2,1)} custom-call(f32[1024,2304]{1,0:T(8,128)} %fusion.x_ref, f32[1,1536]{1,0:T(1,128)} %reshape.64.gain_ref), custom_call_target="tpu_custom_call" | custom-call | flops 15728640 | bytes 9437184 | tf_op jit(solution)/shard_map/norm_heads/pallas_call | solution.py:93
  151.4 1.7 slice.9
  153.1 3.4 pad_maximum_fusion.1
  157.2 123.0 %all-gather.6.cloned.1.call-done.k_ref.v_ref = bf16[4096,1536]{1,0:T(8,128)(2,1)} async-done(((bf16[1024,1536]{1,0:T(8,128)(2,1)}), bf16[4096,1536]{1,0:T(8,128)(2,1)}) %all-gather.6.cloned.1.call-update) | async-done | bytes 12582928 | tf_op jit(solution)/shard_map/all_gather | solution.py:148
  280.2 14.0 %attention.4 = bf16[8,32,768]{2,1,0:T(8,128)(2,1)S(1)} custom-call(bf16[8,128,1536]{2,1,0:T(8,128)(2,1)S(1)} %bitcast.21, bf16[4096,1536]{1,0:T(8,128)(2,1)} %all-gather.6.cloned.1.call-done.k_ref.v_ref, bf16[4096,1536]{1,0:T(8,128)(2,1)} %all-gather.6.cloned.1.call-done.k_ref.v_ref), custom_call_target="tpu_custom_call" | custom-call | flops 3221225472 | bytes 13369344 | tf_op jit(solution)/shard_map/attention/pallas_call | solution.py:64
  294.3 84.1 %all-gather.8.cloned.1.call-done = bf16[6,128,6144]{2,1,0:T(8,128)(2,1)} async-done(((bf16[6,128,1536]{2,1,0:T(8,128)(2,1)}), bf16[6,128,6144]{2,1,0:T(8,128)(2,1)}) %all-gather.8.cloned.1.call-update) | async-done | bytes 9437200 | tf_op jit(solution)/shard_map/all_gather | solution.py:149
  378.3 7.7 %convolution_convert_fusion.3 = bf16[256,6144]{1,0:T(8,128)(2,1)} fusion(bf16[256,768]{1,0:T(8,128)(2,1)S(1)} %bitcast.25, bf16[768,6144]{1,0:T(8,128)(2,1)} %bitcast.30), kind=kOutput, calls=%fused_computation.11 | convolution fusion | flops 2417491968 | bytes 12976128 | tf_op jit(solution)/shard_map/dot_general | solution.py:158
  386.1 14.0 %attention.5 = bf16[8,32,768]{2,1,0:T(8,128)(2,1)S(1)} custom-call(bf16[8,128,1536]{2,1,0:T(8,128)(2,1)S(1)} %bitcast.22, bf16[4096,1536]{1,0:T(8,128)(2,1)} %all-gather.6.cloned.1.call-done.k_ref.v_ref, bf16[4096,1536]{1,0:T(8,128)(2,1)} %all-gather.6.cloned.1.call-done.k_ref.v_ref), custom_call_target="tpu_custom_call" | custom-call | flops 3221225472 | bytes 13369344 | tf_op jit(solution)/shard_map/attention/pallas_call | solution.py:64
  400.1 7.8 %convolution_convert_fusion.2 = bf16[256,6144]{1,0:T(8,128)(2,1)} fusion(bf16[256,768]{1,0:T(8,128)(2,1)S(1)} %bitcast.27, bf16[768,6144]{1,0:T(8,128)(2,1)} %bitcast.31), kind=kOutput, calls=%fused_computation.10 | convolution fusion | flops 2417491968 | bytes 12976128 | tf_op jit(solution)/shard_map/dot_general | solution.py:158
  408.0 14.1 %attention.6 = bf16[8,32,768]{2,1,0:T(8,128)(2,1)S(1)} custom-call(bf16[8,128,1536]{2,1,0:T(8,128)(2,1)S(1)} %bitcast.23, bf16[4096,1536]{1,0:T(8,128)(2,1)} %all-gather.6.cloned.1.call-done.k_ref.v_ref, bf16[4096,1536]{1,0:T(8,128)(2,1)} %all-gather.6.cloned.1.call-done.k_ref.v_ref), custom_call_target="tpu_custom_call" | custom-call | flops 3221225472 | bytes 13369344 | tf_op jit(solution)/shard_map/attention/pallas_call | solution.py:64
  422.0 7.7 %convolution_convert_fusion.1 = bf16[256,6144]{1,0:T(8,128)(2,1)} fusion(bf16[256,768]{1,0:T(8,128)(2,1)S(1)} %bitcast.28, bf16[768,6144]{1,0:T(8,128)(2,1)} %bitcast.32), kind=kOutput, calls=%fused_computation.9 | convolution fusion | flops 2417491968 | bytes 12976128 | tf_op jit(solution)/shard_map/dot_general | solution.py:158
  429.9 14.3 %attention.7 = bf16[8,32,768]{2,1,0:T(8,128)(2,1)S(1)} custom-call(bf16[8,128,1536]{2,1,0:T(8,128)(2,1)S(1)} %bitcast.24, bf16[4096,1536]{1,0:T(8,128)(2,1)} %all-gather.6.cloned.1.call-done.k_ref.v_ref, bf16[4096,1536]{1,0:T(8,128)(2,1)} %all-gather.6.cloned.1.call-done.k_ref.v_ref), custom_call_target="tpu_custom_call" | custom-call | flops 3221225472 | bytes 13369344 | tf_op jit(solution)/shard_map/attention/pallas_call | solution.py:64
  444.2 7.8 %convolution_convert_fusion = bf16[256,6144]{1,0:T(8,128)(2,1)} fusion(bf16[256,768]{1,0:T(8,128)(2,1)S(1)} %bitcast.26, bf16[768,6144]{1,0:T(8,128)(2,1)} %bitcast.33), kind=kOutput, calls=%fused_computation.8 | convolution fusion | flops 2417491968 | bytes 12976128 | tf_op jit(solution)/shard_map/dot_general | solution.py:158
  452.0 16.3 %reduce-scatter.7.cloned.1.call-done = bf16[32,6144]{1,0:T(8,128)(2,1)} async-done(((bf16[256,6144]{1,0:T(8,128)(2,1)}), bf16[32,6144]{1,0:T(8,128)(2,1)}) %reduce-scatter.7.cloned.1.call-update) | async-done | bytes 393232 | tf_op jit(solution)/shard_map/reduce_scatter | solution.py:163
  468.3 41.8 %reduce-scatter.9.cloned.1.call-done = bf16[32,6144]{1,0:T(8,128)(2,1)} async-done(((bf16[256,6144]{1,0:T(8,128)(2,1)}), bf16[32,6144]{1,0:T(8,128)(2,1)}) %reduce-scatter.9.cloned.1.call-update) | async-done | bytes 393232 | tf_op jit(solution)/shard_map/reduce_scatter | solution.py:163
  510.2 42.1 %reduce-scatter.11.cloned.1.call-done = bf16[32,6144]{1,0:T(8,128)(2,1)} async-done(((bf16[256,6144]{1,0:T(8,128)(2,1)}), bf16[32,6144]{1,0:T(8,128)(2,1)}) %reduce-scatter.11.cloned.1.call-update) | async-done | bytes 393232 | tf_op jit(solution)/shard_map/reduce_scatter | solution.py:163
  552.3 2.6 pad_maximum_fusion.3
  (36 shorter events, 6.6 us)
Async XLA Ops:
  6.5 56.7 %all-gather.4.cloned.1.call-start = ((), (), s32[]{:S(2)}) async-start(), calls=%async_computation.4 | async-start | bytes 1769472 | tf_op jit(solution)/shard_map/all_gather | solution.py:121
  7.3 273.0 %all-gather.6.cloned.1.call-start = ((), (), s32[]{:S(2)}) async-start(), calls=%async_computation.5 | async-start | bytes 15728640 | tf_op jit(solution)/shard_map/all_gather | solution.py:148
  11.2 37.0 %copy-start.1 = (bf16[6144]{0:T(1024)(128)(2,1)S(1)}, bf16[6144]{0:T(1024)(128)(2,1)}, u32[]{:S(2)}) copy-start(bf16[6144]{0:T(1024)(128)(2,1)} %param.10) | copy-start | bytes 36868
  11.2 37.0 %copy-start.2 = (f32[2,6,128]{2,0,1:T(2,128)S(1)}, f32[2,6,128]{2,0,1:T(2,128)}, u32[]{:S(2)}) copy-start(f32[2,6,128]{2,0,1:T(2,128)} %param.12) | copy-start | bytes 18436
  151.4 128.9 %copy-start = (bf16[1024,1536]{1,0:T(8,128)(2,1)S(1)}, bf16[1024,1536]{1,0:T(8,128)(2,1)}, u32[]{:S(2)}) copy-start(bf16[1024,1536]{1,0:T(8,128)(2,1)} %norm_heads.1) | copy-start | bytes 9437188
  156.4 221.9 %all-gather.8.cloned.1.call-start = ((), (), s32[]{:S(2)}) async-start(), calls=%async_computation.6 | async-start | bytes 11796480 | tf_op jit(solution)/shard_map/all_gather | solution.py:149
  157.2 294.8 %reduce-scatter.5.cloned.1.call-start = ((), (), s32[]{:S(2)}) async-start(), calls=%async_computation.7 | async-start | bytes 3538944 | tf_op jit(solution)/shard_map/reduce_scatter | solution.py:163
  386.0 82.3 %reduce-scatter.7.cloned.1.call-start = ((), (), s32[]{:S(2)}) async-start(), calls=%async_computation.8 | async-start | bytes 3538944 | tf_op jit(solution)/shard_map/reduce_scatter | solution.py:163
  407.9 102.3 %reduce-scatter.9.cloned.1.call-start = ((), (), s32[]{:S(2)}) async-start(), calls=%async_computation.9 | async-start | bytes 3538944 | tf_op jit(solution)/shard_map/reduce_scatter | solution.py:163
  429.8 122.5 %reduce-scatter.11.cloned.1.call-start = ((), (), s32[]{:S(2)}) async-start(), calls=%async_computation.10 | async-start | bytes 3538944 | tf_op jit(solution)/shard_map/reduce_scatter | solution.py:163
Sparse Core Ops, SparseCore 0:
  8.9 27.9 all-gather.3
  156.6 123.6 all-gather.5
  282.1 96.1 all-gather.7
  386.1 40.3 reduce-scatter.4
  428.7 39.6 reduce-scatter.6
  470.5 39.6 reduce-scatter.8
  512.5 39.7 reduce-scatter.10
where the time goes:
time: 563 us; the launch traced here: 562 us
  waiting for transfers between devices  309 us (55%)
  matrix products  95.3 us (17%)
  Pallas kernels  66.9 us (12%)
  local copies, waits for them, and re-layouts  45.6 us (8%)
  other arithmetic  31.3 us (6%)
  between operations  13.6 us (2%)
    all_gather x1, waiting for transfers between devices, local(): keys_values = lax.all_gather(keys_values, 'row', axis=0, tiled=True)  123 us
    reduce_scatter x4, waiting for transfers between devices, local(): lax.psum_scatter(partial, 'col', scatter_dimension=0, tiled=True)  100 us
    all_gather x1, waiting for transfers between devices, local(): lax.all_gather(w_out, 'row', axis=2, tiled=True)  84.1 us
    pallas_call x4, Pallas kernels, attention(): pl.pallas_call(functools.partial(attention_kernel, key_block, exp_factor)...  56.5 us
    dot_general x1, matrix products, local(): jnp.dot(flat_normed, qkv_matrix, preferred_element_type=jnp.float32)  39 us
    unnamed x8, local copies, waits for them, and re-layouts  37 us
    dot_general x4, matrix products, local(): jnp.dot(context.reshape(col_count * chunk_rows, head_width), out_weight,...  31 us
    dot_general x1, matrix products, local(): jnp.dot(flat_pixels, w_patch, preferred_element_type=jnp.float32) + bias_row  25.3 us
  transfers between devices with their start and end apart: 7, of which 5 were waited for; matrix products, arithmetic and copies ran while one was open for 14% of the time, Pallas kernels for 10%

commit v1 on v0

v1 whole, which is shorter than its diff:
```python
import functools
import math

import jax
import jax.numpy as jnp
from jax import lax
from jax.experimental import pallas as pl
from jax.experimental.pallas import tpu as pltpu
from jax.sharding import PartitionSpec as P

NORM_EPS = 1e-06
KEY_BLOCK = 1024
CHUNKS = 4
MISC = 16
F32 = jnp.float32
BF16 = jnp.bfloat16


def sincos_half(ids, model_width):
    quarter = model_width // 4
    frequency = 1.0 / 10000.0 ** (jnp.arange(quarter, dtype=jnp.float32) / quarter)
    angle = ids.astype(jnp.float32)[:, None] * frequency[None, :]
    return jnp.concatenate([jnp.sin(angle), jnp.cos(angle)], axis=1)


def fold_kernel(group, centred_steps, depth, wp_ref, gain_ref, bias_ref, table_ref, tmean_ref,
                w_ref, f_ref, r_ref, c_ref, a_ref, acc_ref, row_acc):
    step = pl.program_id(0)
    pix, width = wp_ref.shape
    half = width // 2
    grid_rows, grid_cols = r_ref.shape[0], c_ref.shape[0]
    positions = table_ref.shape[0]
    base = pix + MISC

    @pl.when(step == 0)
    def _():
        gain = gain_ref[...]

        def centre(i, carry):
            rows = pl.ds(pl.multiple_of(i * 16, 16), 16)
            w = wp_ref[rows, :].astype(F32)
            mean = jnp.mean(w, axis=1, keepdims=True)
            a_ref[rows, :] = ((w - mean) * gain).astype(BF16)
            return carry

        lax.fori_loop(0, pix // 16, centre, 0)
        bias = bias_ref[...]
        bias = (bias - jnp.mean(bias, axis=1, keepdims=True)) * gain
        high = bias.astype(BF16).astype(F32)
        row = lax.broadcasted_iota(jnp.int32, (MISC, 1), 0)
        misc = jnp.where(row == 0, high, 0.0) + jnp.where(row == 1, bias - high, 0.0)
        a_ref[pix:base, :] = (misc + jnp.where(row == 2, gain, 0.0)).astype(BF16)

        def place(i, carry):
            rows = pl.ds(pl.multiple_of(i * 16, 16), 16)
            to = pl.ds(pl.multiple_of(base + i * 16, 16), 16)
            t = table_ref[rows, :]
            a_ref[to, :half] = (t * gain[:, :half]).astype(BF16)
            a_ref[to, half:] = (t * gain[:, half:]).astype(BF16)
            return carry

        lax.fori_loop(0, positions // 16, place, 0)

    def add(i, carry):
        ks = pl.ds(pl.multiple_of(i * depth, depth), depth)
        w = jnp.concatenate([w_ref[g, ks, :] for g in range(group)], axis=1)
        acc_ref[...] += jnp.dot(a_ref[:, ks], w, preferred_element_type=F32)
        return carry

    acc_ref[...] = jnp.zeros_like(acc_ref)
    lax.fori_loop(0, half // depth, add, 0)
    row_acc[...] = acc_ref[base : base + grid_rows, :]
    acc_ref[base:, :] = jnp.zeros((positions, acc_ref.shape[1]), F32)
    lax.fori_loop(half // depth, width // depth, add, 0)
    bias_w = acc_ref[pix : pix + 1, :] + acc_ref[pix + 1 : pix + 2, :]
    gain_w = acc_ref[pix + 2 : pix + 3, :]
    r = row_acc[...] - tmean_ref[:grid_rows, :] * gain_w
    c = acc_ref[base : base + grid_cols, :] - tmean_ref[:grid_cols, :] * gain_w + bias_w
    f = acc_ref[:pix, :]
    size = f.shape[1] // group
    keep = jnp.where(step < centred_steps, 1.0, 0.0).astype(F32)
    for g in range(group):
        at = slice(g * size, (g + 1) * size)
        for value, out in ((f, f_ref), (r, r_ref), (c, c_ref)):
            part = value[:, at]
            part = part - keep * jnp.mean(part, axis=1, keepdims=True)
            out[:, at] = part.astype(out.dtype)


def fold(w_patch, gain, bias, table, heads_w, heads_here, grid_rows, grid_cols):
    pix, width = w_patch.shape
    total, _, size = heads_w.shape
    group = next(g for g in (2, 3, 1) if heads_here % g == 0)
    steps = total // group
    positions = table.shape[0]
    rows = pix + MISC + positions
    depth = math.gcd(width // 2, 1024)
    tmean = jnp.sum(table, axis=1, keepdims=True) / width
    whole = lambda s: pl.BlockSpec(s, lambda i: (0,) * len(s), pipeline_mode=pl.Buffered(1))
    return pl.pallas_call(
        functools.partial(fold_kernel, group, 2 * heads_here // group, depth),
        grid=(steps,),
        in_specs=[
            whole((pix, width)),
            whole((1, width)),
            whole((1, width)),
            whole(table.shape),
            whole((positions, 1)),
            pl.BlockSpec((group, width, size), lambda i: (i, 0, 0)),
        ],
        out_specs=[
            pl.BlockSpec((pix, group * size), lambda i: (0, i)),
            pl.BlockSpec((grid_rows, group * size), lambda i: (0, i)),
            pl.BlockSpec((grid_cols, group * size), lambda i: (0, i)),
        ],
        out_shape=[
            jax.ShapeDtypeStruct((pix, total * size), BF16),
            jax.ShapeDtypeStruct((grid_rows, total * size), F32),
            jax.ShapeDtypeStruct((grid_cols, total * size), F32),
        ],
        scratch_shapes=[
            pltpu.VMEM((rows, width), BF16),
            pltpu.VMEM((rows, group * size), F32),
            pltpu.VMEM((grid_rows, group * size), F32),
        ],
        compiler_params=pltpu.CompilerParams(
            dimension_semantics=("arbitrary",), vmem_limit_bytes=56 * 1024 * 1024
        ),
        cost_estimate=pl.CostEstimate(
            flops=2 * rows * width * total * size,
            bytes_accessed=2 * width * total * size,
            transcendentals=0,
        ),
        name="fold",
    )(w_patch, gain, bias, table, tmean, heads_w)


def project_kernel(size, normed_width, p_ref, f_ref, r_ref, c_ref, gain_ref, rstd_ref, out_ref):
    lines = r_ref.shape[0]
    cols = c_ref.shape[0]
    width = f_ref.shape[1]
    chunk = 2 * size if width % (2 * size) == 0 and normed_width % (2 * size) == 0 else size
    for line in range(lines):
        rows = slice(line * cols, (line + 1) * cols)
        rstd = rstd_ref[rows, :]
        for start in range(0, width, chunk):
            x = jnp.dot(p_ref[rows, :], f_ref[:, start : start + chunk], preferred_element_type=F32)
            x = x + (c_ref[:, start : start + chunk] + r_ref[line : line + 1, start : start + chunk])
            for at in range(0, chunk, size):
                part = x[:, at : at + size]
                to = slice(start + at, start + at + size)
                if start + at < normed_width:
                    square = jnp.sum(part * part, axis=1, keepdims=True) * (1.0 / size)
                    scale = rstd * lax.rsqrt(square * rstd * rstd + NORM_EPS)
                    part = part * scale * gain_ref[:, to]
                else:
                    part = part * rstd
                out_ref[rows, to] = part.astype(out_ref.dtype)


def project(pixels, f, r, c, gain, rstd, first, width, size, lines):
    tokens, pix = pixels.shape
    cols = c.shape[0]
    at = first // width
    normed_width = gain.shape[1]
    return pl.pallas_call(
        functools.partial(project_kernel, size, normed_width),
        grid=(tokens // (lines * cols),),
        in_specs=[
            pl.BlockSpec((lines * cols, pix), lambda i: (i, 0)),
            pl.BlockSpec((pix, width), lambda i: (0, 0)),
            pl.BlockSpec((lines, width), lambda i: (i, 0)),
            pl.BlockSpec((cols, width), lambda i: (0, 0)),
            pl.BlockSpec((1, normed_width), lambda i: (0, 0)),
            pl.BlockSpec((lines * cols, 1), lambda i: (i, 0)),
        ],
        out_specs=pl.BlockSpec((lines * cols, width), lambda i: (i, 0)),
        out_shape=jax.ShapeDtypeStruct((tokens, width), BF16),
        compiler_params=pltpu.CompilerParams(
            dimension_semantics=("arbitrary",), vmem_limit_bytes=48 * 1024 * 1024
        ),
        cost_estimate=pl.CostEstimate(
            flops=2 * tokens * pix * width, bytes_accessed=4 * tokens * width, transcendentals=tokens
        ),
        name="project",
    )(pixels, f, r, c, gain, rstd)


def attention_kernel(key_block, q_ref, k_ref, v_ref, out_ref):
    rows, head_size = math.prod(q_ref.shape[:-1]), q_ref.shape[-1]
    query = q_ref[...].reshape(rows, head_size)
    peak = jnp.full((rows, 1), -1e30, F32)
    total = jnp.zeros((rows, 1), F32)
    acc = jnp.zeros((rows, head_size), F32)
    for start in range(0, k_ref.shape[0], key_block):
        scores = lax.dot_general(
            query,
            k_ref[start : start + key_block, :],
            (((1,), (1,)), ((), ())),
            preferred_element_type=F32,
        )
        new_peak = jnp.maximum(peak, jnp.max(scores, axis=1, keepdims=True))
        rescale = jnp.exp2(peak - new_peak)
        weights = jnp.exp2(scores - new_peak)
        total = total * rescale + jnp.sum(weights, axis=1, keepdims=True)
        acc = acc * rescale + jnp.dot(
            weights.astype(BF16), v_ref[start : start + key_block, :], preferred_element_type=F32
        )
        peak = new_peak
    out_ref[...] = (acc / total).astype(out_ref.dtype).reshape(out_ref.shape)


def attention(queries, keys_values, chunk, chunk_rows, width, head_size):
    owners = queries.shape[0]
    heads = width // head_size
    key_count = keys_values.shape[0]
    key_block = math.gcd(key_count, KEY_BLOCK)
    rows = owners * chunk_rows
    elements = heads * rows * key_count
    return pl.pallas_call(
        functools.partial(attention_kernel, key_block),
        grid=(heads,),
        in_specs=[
            pl.BlockSpec((owners, chunk_rows, head_size), lambda h: (0, chunk, h)),
            pl.BlockSpec((key_count, head_size), lambda h: (0, h)),
            pl.BlockSpec((key_count, head_size), lambda h: (0, heads + h)),
        ],
        out_specs=pl.BlockSpec((owners, chunk_rows, head_size), lambda h: (0, 0, h)),
        out_shape=jax.ShapeDtypeStruct((owners, chunk_rows, width), BF16),
        compiler_params=pltpu.CompilerParams(
            dimension_semantics=("arbitrary",), vmem_limit_bytes=48 * 1024 * 1024
        ),
        cost_estimate=pl.CostEstimate(
            flops=4 * elements * head_size,
            bytes_accessed=4 * (rows + key_count) * width,
            transcendentals=elements,
        ),
        name="attention",
    )(queries, keys_values, keys_values)


def local(patches, w_patch, patch_bias, ln_gain, w_qkv, qk_gain, w_out):
    tile_rows, tile_cols, pix = patches.shape
    model_width = w_patch.shape[1]
    heads_here, size = w_qkv.shape[2], w_qkv.shape[3]
    head_width = heads_here * size
    col_count, row_count = lax.axis_size("col"), lax.axis_size("row")
    grid_rows, grid_cols = tile_rows * row_count, tile_cols * col_count
    block_tokens = tile_rows * grid_cols
    row_anchor = lax.axis_index("row") * tile_rows
    col_anchor = lax.axis_index("col") * tile_cols

    pixels = lax.all_gather(patches, "col", axis=1, tiled=True)
    pixels = lax.all_gather(pixels, "row", axis=0, tiled=True).reshape(-1, pix)
    out_weight = lax.all_gather(w_out, "row", axis=2, tiled=True).reshape(head_width, model_width)

    bias = patch_bias.astype(F32)[None, :]
    gain = ln_gain.astype(F32)[None, :]
    positions = max(grid_rows, grid_cols)
    table = sincos_half(jnp.arange(positions, dtype=jnp.int32), model_width)
    table = lax.optimization_barrier(table)

    shape = (tile_rows, tile_cols, model_width // 2)
    row_half = lax.dynamic_slice_in_dim(table, row_anchor, tile_rows)
    col_half = lax.dynamic_slice_in_dim(table, col_anchor, tile_cols)
    position = jnp.concatenate(
        [jnp.broadcast_to(row_half[:, None], shape), jnp.broadcast_to(col_half[None], shape)], axis=2
    ).reshape(tile_rows * tile_cols, model_width)
    embedded = jnp.dot(patches.reshape(-1, pix), w_patch, preferred_element_type=F32)
    embedded = embedded + bias + position
    centred = embedded - jnp.mean(embedded, axis=1, keepdims=True)
    variance = jnp.mean(centred * centred, axis=1)
    rstd = lax.rsqrt(variance + NORM_EPS).reshape(tile_rows, tile_cols)
    rstd = lax.all_gather(rstd, "col", axis=1, tiled=True)
    rstd = lax.all_gather(rstd, "row", axis=0, tiled=True).reshape(-1, 1)

    heads_w = w_qkv.transpose(1, 2, 0, 3).reshape(3 * heads_here, model_width, size)
    f, r, c = fold(w_patch, gain, bias, table, heads_w, heads_here, grid_rows, grid_cols)

    q_gain = qk_gain[0].reshape(1, head_width) * (math.log2(math.e) / math.sqrt(size))
    k_gain = qk_gain[1].reshape(1, head_width)
    lines = tile_rows
    keys_values = project(
        pixels, f[:, head_width:], r[:, head_width:], c[:, head_width:], k_gain, rstd, 0,
        2 * head_width, size, lines
    )
    own = row_anchor * grid_cols
    queries = project(
        lax.dynamic_slice_in_dim(pixels, own, block_tokens),
        f[:, :head_width],
        lax.dynamic_slice_in_dim(r[:, :head_width], row_anchor, tile_rows),
        c[:, :head_width], q_gain,
        lax.dynamic_slice_in_dim(rstd, own, block_tokens), 0, head_width, size, lines
    )
    owned = block_tokens // col_count
    chunk_rows = owned // math.gcd(owned // 16, CHUNKS)
    queries = queries.reshape(col_count, owned, head_width)
    pieces = []
    for chunk in range(owned // chunk_rows):
        context = attention(queries, keys_values, chunk, chunk_rows, head_width, size)
        partial = jnp.dot(
            context.reshape(col_count * chunk_rows, head_width), out_weight,
            preferred_element_type=F32,
        ).astype(BF16)
        pieces.append(lax.psum_scatter(partial, "col", scatter_dimension=0, tiled=True))
    return jnp.concatenate(pieces, axis=0)


def solution(mesh):
    return jax.shard_map(
        local,
        mesh=mesh,
        in_specs=(
            P("row", "col", None),
            P(),
            P(),
            P(),
            P(None, None, "col", None),
            P(None, "col", None),
            P("col", None, "row"),
        ),
        out_specs=P(("row", "col"), None),
        check_vma=False,
    )
```

time: 563 us -> 390 us (0.69)
  waiting for transfers between devices: 309 us -> 162 us
  Pallas kernels: 66.9 us -> 131 us
  matrix products: 95.3 us -> 36.3 us
  local copies, waits for them, and re-layouts: 45.6 us -> 16.2 us
  other arithmetic: 31.3 us -> 7.67 us
  blocking collectives: 0 us -> 22.9 us
    all_gather x1, waiting for transfers between devices: 123 us -> 0.02 us  [local(): pixels = lax.all_gather(pixels, 'row', axis=0, tiled=True).reshape(-1, pix)]
    pallas_call x5 -> x7, Pallas kernels: 66.9 us -> 131 us  [the longest x1 56.6 us: fold(): pl.pallas_call(functools.partial(fold_kernel, group, 2 * heads_here // gr...]
    dot_general x2 -> x1, matrix products: 64.3 us -> 5.28 us  [local(): jnp.dot(patches.reshape(-1, pix), w_patch, preferred_element_type=F32)]
    all_gather x1, waiting for transfers between devices: 84.1 us -> 28.2 us  [local(): lax.all_gather(w_out, 'row', axis=2, tiled=True)]
    unnamed x8 -> x25, local copies, waits for them, and re-layouts: 37 us -> 1.93 us
    all_gather x1, waiting for transfers between devices: 0.01 us -> 29.7 us  [local(): pixels = lax.all_gather(patches, 'col', axis=1, tiled=True)]
    all_gather x0 -> x2, blocking collectives: none -> 22.9 us  [the longest x1 14.1 us: local(): rstd = lax.all_gather(rstd, 'col', axis=1, tiled=True)]
    concatenate x2 -> x1, other arithmetic: 14.6 us -> 0.24 us  [local(): jnp.concatenate([jnp.broadcast_to(row_half[:, None], shape), jnp.broadcas...]
  transfers between devices with their start and end apart: 7 -> 7, of which waited for: 5 -> 5; matrix products, arithmetic and copies ran while one was open for 14% -> 12% of each run, Pallas kernels for 10% -> 34%
where the time goes in v1:
time: 390 us
  waiting for transfers between devices  162 us (42%)
  Pallas kernels  131 us (34%)
  matrix products  36.3 us (9%)
  blocking collectives  22.9 us (6%)
  local copies, waits for them, and re-layouts  16.2 us (4%)
  between operations  13.7 us (4%)
  other arithmetic  7.67 us (2%)
    reduce_scatter x4, waiting for transfers between devices, local(): lax.psum_scatter(partial, 'col', scatter_dimension=0, tiled=True)  102 us
    pallas_call x1, Pallas kernels, fold(): pl.pallas_call(functools.partial(fold_kernel, group, 2 * heads_here // gr...  56.6 us
    pallas_call x4, Pallas kernels, attention(): pl.pallas_call(functools.partial(attention_kernel, key_block), grid=(head...  54 us
    dot_general x4, matrix products, local(): jnp.dot(context.reshape(col_count * chunk_rows, head_width), out_weight,...  31 us
    all_gather x1, waiting for transfers between devices, local(): pixels = lax.all_gather(patches, 'col', axis=1, tiled=True)  29.7 us
    all_gather x1, waiting for transfers between devices, local(): lax.all_gather(w_out, 'row', axis=2, tiled=True)  28.2 us
    pallas_call x2, Pallas kernels, project(): pl.pallas_call(functools.partial(project_kernel, size, normed_width), gri...  20.5 us
    all_gather x1, blocking collectives, local(): rstd = lax.all_gather(rstd, 'col', axis=1, tiled=True)  14.1 us
  transfers between devices with their start and end apart: 7, of which 5 were waited for; matrix products, arithmetic and copies ran while one was open for 12% of the time, Pallas kernels for 34%

profile of v1, /device:TPU:0, one launch (start us, length us, event | category | flops | bytes accessed | tf_op | source)
XLA Modules:
  0.0 389.8 jit_solution(13606144873410325325)
XLA Ops:
  7.3 29.7 %all-gather.5.cloned.1.call-done = bf16[8,128,768]{2,1,0:T(8,128)(2,1)} async-done(((bf16[8,16,768]{2,1,0:T(8,128)(2,1)}), bf16[8,128,768]{2,1,0:T(8,128)(2,1)}) %all-gather.5.cloned.1.call-update) | async-done | bytes 1572880 | tf_op jit(solution)/shard_map/all_gather | solution.py:253
  39.0 2.8 multiply_sine_fusion
  43.1 56.6 %fold.1 = (bf16[768,2304]{1,0:T(8,128)(2,1)}, f32[32,2304]{1,0:T(8,128)}, f32[128,2304]{1,0:T(8,128)}) custom-call(bf16[768,6144]{1,0:T(8,128)(2,1)} %wp_ref.1, f32[1,6144]{1,0:T(1,128)} %bitcast.51, f32[1,6144]{1,0:T(1,128)} %bitcast.49, f32[128,3072]{1,0:T(8,128)} %copy-done.4, f32[128,1]{1,0:T(8,128)} %copy.13.tmean_ref, bf16[18,6144,128]{2,1,0:T(8,128)(2,1)} %bitcast.54), custom_call_target="tpu_custom_call" | custom-call | flops 25820135424 | bytes 28311552 | tf_op jit(solution)/shard_map/fold/pallas_call | solution.py:100
  101.1 3.3 slice.28.f_ref
  109.3 5.3 %fusion.1 = (f32[128]{0:T(128)S(1)}, f32[128,6144]{1,0:T(8,128)S(1)}) fusion(f32[128,6144]{1,0:T(8,128)S(1)} %bitcast.45, f32[6144]{0:T(1024)S(1)} %copy-done.8, bf16[128,768]{1,0:T(8,128)(2,1)S(1)} %bitcast.46, bf16[768,6144]{1,0:T(8,128)(2,1)} %wp_ref.1), kind=kOutput, calls=%fused_computation.24 | convolution fusion | flops 1210318720 | bytes 15950336 | tf_op jit(solution)/shard_map/dot_general | solution.py:269
  115.2 14.1 %all-gather = f32[8,16,8]{1,2,0:T(8,128)S(1)} all-gather(f32[1,16,8]{1,2,0:T(8,128)S(1)} %bitcast.53), channel_id=1, replica_groups=mesh['row'=4,'col'=8] {'col'}, dimensions={0}, use_global_device_ids=true | all-gather | bytes 4608 | tf_op jit(solution)/shard_map/all_gather | solution.py:274
  129.4 8.8 %all_gather.18 = f32[32,128]{1,0:T(8,128)S(1)} all-gather(f32[8,128]{1,0:T(8,128)S(1)} %bitcast.52), channel_id=1, replica_groups=mesh['row'=4,'col'=8] {'row'}, dimensions={0}, use_global_device_ids=true | all-gather | bytes 20480 | tf_op jit(solution)/shard_map/all_gather | solution.py:275
  138.2 2.0 copy.15.rstd_ref
  141.3 1.5 constant_dynamic-slice_fusion.4.p_ref
  144.0 2.5 project.2
  146.5 18.0 %project.3.k_ref.v_ref = bf16[4096,1536]{1,0:T(8,128)(2,1)} custom-call(bf16[4096,768]{1,0:T(8,128)(2,1)} %bitcast.48, bf16[768,1536]{1,0:T(8,128)(2,1)S(1)} %copy-done.1, f32[32,1536]{1,0:T(8,128)S(1)} %slice.29.r_ref, f32[128,1536]{1,0:T(8,128)S(1)} %copy-done.3, f32[1,768]{1,0:T(1,128)S(1)} %get-tuple-element.13.gain_ref, f32[4096,1]{1,0:T(8,128)S(1)} %copy-done), custom_call_target="tpu_custom_call" | custom-call | flops 9663676416 | bytes 25165824 | tf_op jit(solution)/shard_map/project/pallas_call | solution.py:166
  164.5 13.5 %attention.7 = bf16[8,32,768]{2,1,0:T(8,128)(2,1)S(1)} custom-call(bf16[8,128,768]{2,1,0:T(8,128)(2,1)S(1)} %bitcast.37, bf16[4096,1536]{1,0:T(8,128)(2,1)} %project.3.k_ref.v_ref, bf16[4096,1536]{1,0:T(8,128)(2,1)} %project.3.k_ref.v_ref), custom_call_target="tpu_custom_call" | custom-call | flops 3221225472 | bytes 13369344 | tf_op jit(solution)/shard_map/attention/pallas_call | solution.py:220
  178.0 28.2 %all-gather.9.cloned.1.call-done = bf16[6,128,6144]{2,1,0:T(8,128)(2,1)} async-done(((bf16[6,128,1536]{2,1,0:T(8,128)(2,1)}), bf16[6,128,6144]{2,1,0:T(8,128)(2,1)}) %all-gather.9.cloned.1.call-update) | async-done | bytes 9437200 | tf_op jit(solution)/shard_map/all_gather | solution.py:255
  206.2 7.7 %convolution_convert_fusion = bf16[256,6144]{1,0:T(8,128)(2,1)} fusion(bf16[256,768]{1,0:T(8,128)(2,1)S(1)} %bitcast.41, bf16[768,6144]{1,0:T(8,128)(2,1)} %bitcast.55), kind=kOutput, calls=%fused_computation | convolution fusion | flops 2417491968 | bytes 12976128 | tf_op jit(solution)/shard_map/dot_general | solution.py:301
  214.2 13.5 %attention.6 = bf16[8,32,768]{2,1,0:T(8,128)(2,1)S(1)} custom-call(bf16[8,128,768]{2,1,0:T(8,128)(2,1)S(1)} %bitcast.38, bf16[4096,1536]{1,0:T(8,128)(2,1)} %project.3.k_ref.v_ref, bf16[4096,1536]{1,0:T(8,128)(2,1)} %project.3.k_ref.v_ref), custom_call_target="tpu_custom_call" | custom-call | flops 3221225472 | bytes 13369344 | tf_op jit(solution)/shard_map/attention/pallas_call | solution.py:220
  227.7 7.8 %convolution_convert_fusion.1 = bf16[256,6144]{1,0:T(8,128)(2,1)} fusion(bf16[256,768]{1,0:T(8,128)(2,1)S(1)} %bitcast.43, bf16[768,6144]{1,0:T(8,128)(2,1)} %bitcast.56), kind=kOutput, calls=%fused_computation.1 | convolution fusion | flops 2417491968 | bytes 12976128 | tf_op jit(solution)/shard_map/dot_general | solution.py:301
  235.5 13.5 %attention.5 = bf16[8,32,768]{2,1,0:T(8,128)(2,1)S(1)} custom-call(bf16[8,128,768]{2,1,0:T(8,128)(2,1)S(1)} %bitcast.39, bf16[4096,1536]{1,0:T(8,128)(2,1)} %project.3.k_ref.v_ref, bf16[4096,1536]{1,0:T(8,128)(2,1)} %project.3.k_ref.v_ref), custom_call_target="tpu_custom_call" | custom-call | flops 3221225472 | bytes 13369344 | tf_op jit(solution)/shard_map/attention/pallas_call | solution.py:220
  249.0 7.7 %convolution_convert_fusion.2 = bf16[256,6144]{1,0:T(8,128)(2,1)} fusion(bf16[256,768]{1,0:T(8,128)(2,1)S(1)} %bitcast.44, bf16[768,6144]{1,0:T(8,128)(2,1)} %bitcast.57), kind=kOutput, calls=%fused_computation.2 | convolution fusion | flops 2417491968 | bytes 12976128 | tf_op jit(solution)/shard_map/dot_general | solution.py:301
  256.8 13.5 %attention.4 = bf16[8,32,768]{2,1,0:T(8,128)(2,1)S(1)} custom-call(bf16[8,128,768]{2,1,0:T(8,128)(2,1)S(1)} %bitcast.40, bf16[4096,1536]{1,0:T(8,128)(2,1)} %project.3.k_ref.v_ref, bf16[4096,1536]{1,0:T(8,128)(2,1)} %project.3.k_ref.v_ref), custom_call_target="tpu_custom_call" | custom-call | flops 3221225472 | bytes 13369344 | tf_op jit(solution)/shard_map/attention/pallas_call | solution.py:220
  270.3 7.8 %convolution_convert_fusion.3 = bf16[256,6144]{1,0:T(8,128)(2,1)} fusion(bf16[256,768]{1,0:T(8,128)(2,1)S(1)} %bitcast.42, bf16[768,6144]{1,0:T(8,128)(2,1)} %bitcast.58), kind=kOutput, calls=%fused_computation.3 | convolution fusion | flops 2417491968 | bytes 12976128 | tf_op jit(solution)/shard_map/dot_general | solution.py:301
  278.2 18.2 %reduce-scatter.9.cloned.1.call-done = bf16[32,6144]{1,0:T(8,128)(2,1)} async-done(((bf16[256,6144]{1,0:T(8,128)(2,1)}), bf16[32,6144]{1,0:T(8,128)(2,1)}) %reduce-scatter.9.cloned.1.call-update) | async-done | bytes 393232 | tf_op jit(solution)/shard_map/reduce_scatter | solution.py:305
  296.4 41.8 %reduce-scatter.7.cloned.1.call-done = bf16[32,6144]{1,0:T(8,128)(2,1)} async-done(((bf16[256,6144]{1,0:T(8,128)(2,1)}), bf16[32,6144]{1,0:T(8,128)(2,1)}) %reduce-scatter.7.cloned.1.call-update) | async-done | bytes 393232 | tf_op jit(solution)/shard_map/reduce_scatter | solution.py:305
  338.2 42.1 %reduce-scatter.5.cloned.1.call-done = bf16[32,6144]{1,0:T(8,128)(2,1)} async-done(((bf16[256,6144]{1,0:T(8,128)(2,1)}), bf16[32,6144]{1,0:T(8,128)(2,1)}) %reduce-scatter.5.cloned.1.call-update) | async-done | bytes 393232 | tf_op jit(solution)/shard_map/reduce_scatter | solution.py:305
  380.3 2.6 pad_maximum_fusion.2
  (67 shorter events, 13.6 us)
Async XLA Ops:
  6.5 31.2 %copy-start.9 = (bf16[6144]{0:T(1024)(128)(2,1)S(1)}, bf16[6144]{0:T(1024)(128)(2,1)}, u32[]{:S(2)}) copy-start(bf16[6144]{0:T(1024)(128)(2,1)} %param.10) | copy-start | bytes 36868
  6.5 31.9 %copy-start.10 = (bf16[6144]{0:T(1024)(128)(2,1)S(1)}, bf16[6144]{0:T(1024)(128)(2,1)}, u32[]{:S(2)}) copy-start(bf16[6144]{0:T(1024)(128)(2,1)} %param.9) | copy-start | bytes 36868
  6.5 30.4 %all-gather.5.cloned.1.call-start = ((), (), s32[]{:S(2)}) async-start(), calls=%async_computation.4 | async-start | bytes 1769472 | tf_op jit(solution)/shard_map/all_gather | solution.py:253
  7.3 134.0 %all-gather.7.cloned.1.call-start = ((), (), s32[]{:S(2)}) async-start(), calls=%async_computation.5 | async-start | bytes 7864320 | tf_op jit(solution)/shard_map/all_gather | solution.py:254
  37.0 169.2 %all-gather.9.cloned.1.call-start = ((), (), s32[]{:S(2)}) async-start(), calls=%async_computation.6 | async-start | bytes 11796480 | tf_op jit(solution)/shard_map/all_gather | solution.py:255
  37.7 240.4 %reduce-scatter.11.cloned.1.call-start = ((), (), s32[]{:S(2)}) async-start(), calls=%async_computation.10 | async-start | bytes 3538944 | tf_op jit(solution)/shard_map/reduce_scatter | solution.py:305
  41.9 1.1 copy-start.4
  99.7 4.7 %copy-start.7 = (f32[32,2304]{1,0:T(8,128)S(1)}, f32[32,2304]{1,0:T(8,128)}, u32[]{:S(2)}) copy-start(f32[32,2304]{1,0:T(8,128)} %get-tuple-element.9) | copy-start | bytes 884740
  101.1 3.4 copy-start.5
  108.4 0.9 copy-start.6
  108.4 0.9 copy-start.8
  114.6 26.6 %copy-start.11 = (f32[2,6,128]{2,0,1:T(2,128)S(1)}, f32[2,6,128]{2,0,1:T(2,128)}, u32[]{:S(2)}) copy-start(f32[2,6,128]{2,0,1:T(2,128)} %param.12) | copy-start | bytes 18436
  142.8 3.7 copy-start
  142.8 3.7 copy-start.1
  142.8 1.1 copy-start.2
  144.0 2.5 copy-start.3
  213.9 82.5 %reduce-scatter.9.cloned.1.call-start = ((), (), s32[]{:S(2)}) async-start(), calls=%async_computation.9 | async-start | bytes 3538944 | tf_op jit(solution)/shard_map/reduce_scatter | solution.py:305
  235.5 102.8 %reduce-scatter.7.cloned.1.call-start = ((), (), s32[]{:S(2)}) async-start(), calls=%async_computation.8 | async-start | bytes 3538944 | tf_op jit(solution)/shard_map/reduce_scatter | solution.py:305
  256.8 123.5 %reduce-scatter.5.cloned.1.call-start = ((), (), s32[]{:S(2)}) async-start(), calls=%async_computation.7 | async-start | bytes 3538944 | tf_op jit(solution)/shard_map/reduce_scatter | solution.py:305
Sparse Core Ops, SparseCore 0:
  8.9 27.9 all-gather.4
  38.8 69.1 all-gather.6
  109.8 96.2 all-gather.8
  214.0 40.3 reduce-scatter.10
  256.6 39.7 reduce-scatter.8
  298.5 39.6 reduce-scatter.6
  340.5 39.7 reduce-scatter.4

commit v2 on v1

v2 whole, which is shorter than its diff:
```python
import functools
import math

import jax
import jax.numpy as jnp
from jax import lax
from jax.experimental import pallas as pl
from jax.experimental.pallas import tpu as pltpu
from jax.sharding import PartitionSpec as P

NORM_EPS = 1e-06
KEY_BLOCK = 1024
CHUNKS = 4
MISC = 16
F32 = jnp.float32
BF16 = jnp.bfloat16


def sincos_half(ids, model_width):
    quarter = model_width // 4
    frequency = 1.0 / 10000.0 ** (jnp.arange(quarter, dtype=jnp.float32) / quarter)
    angle = ids.astype(jnp.float32)[:, None] * frequency[None, :]
    return jnp.concatenate([jnp.sin(angle), jnp.cos(angle)], axis=1)


def ids():
    row, col = lax.axis_index("row"), lax.axis_index("col")
    return row, col, lax.div(col, 2), lax.rem(col, 2)


def row_peer(row, hop, count):
    if count != 4:
        return lax.rem(row + hop, count)
    if hop == 1:
        return row + 1 - 2 * lax.rem(row, 2)
    if hop == 2:
        return lax.rem(row + 2, 4)
    return 3 - row


def remote(src, dst, send, recv, row, col):
    return pltpu.make_async_remote_copy(
        src_ref=src, dst_ref=dst, send_sem=send, recv_sem=recv,
        device_id=(row, col), device_id_type=pl.DeviceIdType.MESH,
    )


def prep_kernel(sizes, group, centred_steps, patch_ref, wp_ref, gain_ref, bias_ref, table_ref,
                tmean_ref, w_ref, f_ref, r_ref, c_ref, pixels_ref, rstd_ref,
                a_ref, acc_ref, row_acc, e_ref, mine_ref, seen_ref,
                local_sem, send_sem, recv_sem, stat_send, stat_recv):
    row_count, col_count, tile_rows, tile_cols = sizes
    step = pl.program_id(0)
    last = pl.num_programs(0) - 1
    pix, width = wp_ref.shape
    half = width // 2
    grid_rows, grid_cols = r_ref.shape[0], c_ref.shape[0]
    positions = table_ref.shape[0]
    base = pix + MISC
    tokens = tile_rows * tile_cols
    row, col, line, core = ids()
    me = row * col_count + col
    devices = row_count * col_count
    lines = col_count // 2
    partner = 2 * line + 1 - core

    def give(src, block, to_row, to_col):
        remote(src, pixels_ref.at[block], send_sem, recv_sem.at[block], to_row, to_col).start()

    def got(block):
        pltpu.make_async_copy(pixels_ref.at[block], pixels_ref.at[block], recv_sem.at[block]).wait()

    def to_rows(src, block):
        for hop in range(1, row_count):
            give(src, block, row_peer(row, hop, row_count), col)

    @pl.when(step == 0)
    def _():
        for hop in range(1, lines):
            give(patch_ref, me, row, 2 * lax.rem(line + hop, lines) + core)
        to_rows(patch_ref, me)
        give(patch_ref, me, row, partner)
        pltpu.make_async_copy(patch_ref, pixels_ref.at[me], local_sem).start()
        gain = gain_ref[...]

        def centre(i, carry):
            rows = pl.ds(pl.multiple_of(i * 16, 16), 16)
            w = wp_ref[rows, :].astype(F32)
            mean = jnp.sum(w, axis=1, keepdims=True) * (1.0 / width)
            a_ref[rows, :] = ((w - mean) * gain).astype(BF16)
            return carry

        lax.fori_loop(0, pix // 16, centre, 0)
        bias = bias_ref[...]
        bias = (bias - jnp.mean(bias, axis=1, keepdims=True)) * gain
        high = bias.astype(BF16).astype(F32)
        at = lax.broadcasted_iota(jnp.int32, (MISC, 1), 0)
        misc = jnp.where(at == 0, high, 0.0) + jnp.where(at == 1, bias - high, 0.0)
        a_ref[pix:base, :] = (misc + jnp.where(at == 2, gain, 0.0)).astype(BF16)

        def place(i, carry):
            rows = pl.ds(pl.multiple_of(i * 16, 16), 16)
            to = pl.ds(pl.multiple_of(base + i * 16, 16), 16)
            t = table_ref[rows, :]
            a_ref[to, :half] = (t * gain[:, :half]).astype(BF16)
            a_ref[to, half:] = (t * gain[:, half:]).astype(BF16)
            return carry

        lax.fori_loop(0, positions // 16, place, 0)

    @pl.when(step == 1)
    def _():
        chunk = math.gcd(half, 512)
        own_rows = pl.ds(pl.multiple_of(row * tile_rows, 8), tile_rows)
        own_cols = pl.ds(pl.multiple_of(col * tile_cols, 8), tile_cols)
        shape = (tile_rows, tile_cols, chunk)

        def embed(i, carry):
            for side in range(2):
                at = pl.ds(pl.multiple_of(i * chunk, chunk), chunk)
                to = pl.ds(pl.multiple_of(side * half + i * chunk, chunk), chunk)
                if side == 0:
                    t = jnp.broadcast_to(table_ref[own_rows, at][:, None, :], shape)
                else:
                    t = jnp.broadcast_to(table_ref[own_cols, at][None, :, :], shape)
                e = jnp.dot(patch_ref[...], wp_ref[:, to], preferred_element_type=F32)
                e_ref[:, to] = e + bias_ref[:, to] + t.reshape(tokens, chunk)
            return carry

        lax.fori_loop(0, half // chunk, embed, 0)
        mean = jnp.sum(e_ref[...], axis=1, keepdims=True) * (1.0 / width)
        centred = e_ref[...] - mean
        variance = jnp.sum(centred * centred, axis=1, keepdims=True) * (1.0 / width)
        rstd = jnp.broadcast_to(lax.rsqrt(variance + NORM_EPS), (tokens, 128))
        mine_ref[...] = rstd.T[:8, :]

        def tell(hop, carry):
            to = lax.rem(me + hop, devices)
            remote(mine_ref, seen_ref.at[hop - 1], stat_send, stat_recv,
                   lax.div(to, col_count), lax.rem(to, col_count)).start()
            return carry

        lax.fori_loop(1, devices, tell, 0)
        seen_ref[devices - 1] = mine_ref[...]

    @pl.when(step == jnp.minimum(3, last))
    def _():
        for hop in range(1, lines):
            block = row * col_count + 2 * lax.rem(line + hop, lines) + core
            got(block)
            to_rows(pixels_ref.at[block], block)
            give(pixels_ref.at[block], block, row, partner)

    def product(start):
        ks = slice(start, start + half)
        w = jnp.concatenate([w_ref[g, ks, :] for g in range(group)], axis=1)
        return jnp.dot(a_ref[:, ks], w, preferred_element_type=F32)

    acc_ref[...] = product(0)
    row_acc[...] = acc_ref[base : base + grid_rows, :]
    acc_ref[base:, :] = jnp.zeros((positions, acc_ref.shape[1]), F32)
    acc_ref[...] += product(half)
    bias_w = acc_ref[pix : pix + 1, :] + acc_ref[pix + 1 : pix + 2, :]
    gain_w = acc_ref[pix + 2 : pix + 3, :]
    r = row_acc[...] - tmean_ref[:grid_rows, :] * gain_w
    c = acc_ref[base : base + grid_cols, :] - tmean_ref[:grid_cols, :] * gain_w + bias_w
    f = acc_ref[:pix, :]
    size = f.shape[1] // group
    keep = jnp.where(step < centred_steps, 1.0, 0.0).astype(F32)
    for g in range(group):
        at = slice(g * size, (g + 1) * size)
        for value, out in ((f, f_ref), (r, r_ref), (c, c_ref)):
            part = value[:, at]
            part = part - keep * jnp.mean(part, axis=1, keepdims=True)
            out[:, at] = part.astype(out.dtype)

    @pl.when(step == last)
    def _():
        for hop in range(1, row_count):
            for i in range(lines):
                block = row_peer(row, hop, row_count) * col_count + 2 * i + core
                got(block)
                give(pixels_ref.at[block], block, row, partner)
        for other in range(row_count):
            for i in range(lines):
                got(other * col_count + 2 * i + 1 - core)
        everyone = pixels_ref.at[pl.ds(0, devices - 1)]
        pltpu.make_async_copy(everyone, everyone, send_sem).wait()
        pltpu.make_async_copy(patch_ref, pixels_ref.at[me], local_sem).wait()
        seen = seen_ref.at[pl.ds(0, devices - 1)]
        pltpu.make_async_copy(seen, seen, stat_recv).wait()
        pltpu.make_async_copy(seen, seen, stat_send).wait()

        def put(block, carry):
            rstd_ref[block] = seen_ref[lax.rem(me - block + 2 * devices - 1, devices)]
            return carry

        lax.fori_loop(0, devices, put, 0)


def prep(patches, w_patch, gain, bias, table, heads_w, sizes, heads_here, grid_rows, grid_cols):
    pix, width = w_patch.shape
    total, _, size = heads_w.shape
    group = next(g for g in (2, 3, 1) if heads_here % g == 0)
    steps = total // group
    positions = table.shape[0]
    rows = pix + MISC + positions
    tokens = patches.shape[0]
    devices = sizes[0] * sizes[1]
    tmean = jnp.sum(table, axis=1, keepdims=True) / width
    whole = lambda s: pl.BlockSpec(s, lambda i: (0,) * len(s), pipeline_mode=pl.Buffered(1))
    return pl.pallas_call(
        functools.partial(prep_kernel, sizes, group, 2 * heads_here // group),
        grid=(steps,),
        in_specs=[
            whole((tokens, pix)),
            whole((pix, width)),
            whole((1, width)),
            whole((1, width)),
            whole(table.shape),
            whole((positions, 1)),
            pl.BlockSpec((group, width, size), lambda i: (i, 0, 0)),
        ],
        out_specs=[
            pl.BlockSpec((pix, group * size), lambda i: (0, i)),
            pl.BlockSpec((grid_rows, group * size), lambda i: (0, i)),
            pl.BlockSpec((grid_cols, group * size), lambda i: (0, i)),
            pl.BlockSpec(memory_space=pl.ANY),
            pl.BlockSpec((devices, 8, tokens), lambda i: (0, 0, 0)),
        ],
        out_shape=[
            jax.ShapeDtypeStruct((pix, total * size), BF16),
            jax.ShapeDtypeStruct((grid_rows, total * size), F32),
            jax.ShapeDtypeStruct((grid_cols, total * size), F32),
            jax.ShapeDtypeStruct((devices, tokens, pix), BF16),
            jax.ShapeDtypeStruct((devices, 8, tokens), F32),
        ],
        scratch_shapes=[
            pltpu.VMEM((rows, width), BF16),
            pltpu.VMEM((rows, group * size), F32),
            pltpu.VMEM((grid_rows, group * size), F32),
            pltpu.VMEM((tokens, width), F32),
            pltpu.VMEM((8, tokens), F32),
            pltpu.VMEM((devices, 8, tokens), F32),
            pltpu.SemaphoreType.DMA,
            pltpu.SemaphoreType.DMA,
            pltpu.SemaphoreType.DMA((devices,)),
            pltpu.SemaphoreType.DMA,
            pltpu.SemaphoreType.DMA,
        ],
        compiler_params=pltpu.CompilerParams(
            dimension_semantics=("arbitrary",), vmem_limit_bytes=60 * 1024 * 1024,
            has_side_effects=True,
        ),
        cost_estimate=pl.CostEstimate(
            flops=2 * rows * width * total * size,
            bytes_accessed=2 * width * total * size,
            transcendentals=0,
        ),
        name="prep",
    )(patches, w_patch, gain, bias, table, tmean, heads_w)

def attention_block(key_block, query, k_ref, v_ref):
    rows, head_size = query.shape
    peak = jnp.full((rows, 1), -1e30, F32)
    total = jnp.zeros((rows, 1), F32)
    acc = jnp.zeros((rows, head_size), F32)
    for start in range(0, k_ref.shape[0], key_block):
        scores = lax.dot_general(
            query,
            k_ref[start : start + key_block, :],
            (((1,), (1,)), ((), ())),
            preferred_element_type=F32,
        )
        new_peak = jnp.maximum(peak, jnp.max(scores, axis=1, keepdims=True))
        rescale = jnp.exp2(peak - new_peak)
        weights = jnp.exp2(scores - new_peak)
        total = total * rescale + jnp.sum(weights, axis=1, keepdims=True)
        acc = acc * rescale + jnp.dot(
            weights.astype(BF16), v_ref[start : start + key_block, :], preferred_element_type=F32
        )
        peak = new_peak
    return (acc / total).astype(BF16)


def attend_kernel(sizes, heads, key_block, pixels_ref, f_ref, r_ref, c_ref, gain_ref, rstd_ref,
                  rq_ref, w_ref, out_ref, kv_ref, wall_ref, pbuf_ref, qbuf_ref, q_ref, ctx_ref,
                  pair_ref, hop_ref, own_ref, stage_ref, w_local, w_send, w_recv, p_sem, q_sem,
                  stage_send, pair_recv, hop_send, hop_recv):
    row_count, col_count, tile_rows, tile_cols = sizes
    row, col, line, core = ids()
    lines = col_count // 2
    partner = 2 * line + 1 - core
    size = kv_ref.shape[2]
    head_width = heads * size
    blocks, tokens, pix = pbuf_ref.shape[1:]
    owned = tile_cols * tile_rows
    per_line = tile_cols * col_count // owned
    part = wall_ref.shape[2]
    wide = 2 * size
    is_end = jnp.logical_or(line == 0, line == lines - 1)

    def wait(ref, sem):
        pltpu.make_async_copy(ref, ref, sem).wait()

    def order(s):
        up = jnp.where(s < lines - 1 - line, lines - 1 - s, s - (lines - 1 - line))
        down = jnp.where(s < line, s, lines - 1 - (s - line))
        far = jnp.where(2 * line < lines, up, down)
        return jnp.where(s == lines - 1, line, far)

    relay = row_count == 4
    piece = part // 2

    def relayed(side):
        at = pl.ds(side * piece, piece)
        return remote(wall_ref.at[1 + side, :, at], wall_ref.at[3, :, at], w_send.at[3 + side],
                      w_recv.at[3 + side], row_peer(row, 2 - side, row_count), col)

    for hop in range(1, 3 if relay else row_count):
        remote(w_ref, wall_ref.at[hop], w_send.at[hop], w_recv.at[hop],
               row_peer(row, hop, row_count), col).start()
    pltpu.make_async_copy(w_ref, wall_ref.at[0], w_local).start()

    def fetch(i):
        slot = lax.rem(i, 2)
        return pltpu.make_async_copy(
            pixels_ref.at[pl.ds(i * blocks, blocks)], pbuf_ref.at[slot], p_sem.at[slot]
        )

    def q_row(s, side):
        return 2 * order(s) + (core if side else 1 - core)

    def fetch_q(s):
        for side in range(2):
            mine = q_row(s, side)
            first = lax.rem(mine, per_line) * tile_rows
            lane = pl.multiple_of(lax.div(mine, per_line) * tile_cols, tile_cols)
            for c in range(tile_rows):
                pltpu.make_async_copy(
                    pixels_ref.at[row * col_count + first + c, pl.ds(lane, tile_cols), :],
                    qbuf_ref.at[pl.ds(side * owned + c * tile_cols, tile_cols), :],
                    q_sem,
                ).start()

    def pick(rows, index):
        at = lax.broadcasted_iota(jnp.int32, rows.shape, 0)
        return jnp.sum(jnp.where(at == index, rows, 0.0), axis=0, keepdims=True)

    def normed(x, scale_rows, gain):
        square = jnp.sum(x * x, axis=1, keepdims=True) * (1.0 / size)
        return x * (scale_rows * lax.rsqrt(square * scale_rows * scale_rows + NORM_EPS)) * gain

    fetch(0).start()
    fetch_q(0)
    rounds = pixels_ref.shape[0] // blocks

    def keys_values(i, carry):
        fetch(i).wait()

        @pl.when(i + 1 < rounds)
        def _():
            fetch(i + 1).start()

        p = pbuf_ref[lax.rem(i, 2)].reshape(blocks * tokens, pix)
        rstd = []
        for b in range(blocks):
            lanes = rstd_ref[i * blocks + b][0:1, :]
            rstd.append(jnp.broadcast_to(lanes, (size, tokens)).T)
        for start in range(0, 2 * head_width, wide):
            at = slice(head_width + start, head_width + start + wide)
            x = jnp.dot(p, f_ref[:, at], preferred_element_type=F32)
            for b in range(blocks):
                block = i * blocks + b
                rows = pl.ds(pl.multiple_of(lax.div(block, col_count) * tile_rows, 8), tile_rows)
                cols = pl.ds(pl.multiple_of(lax.rem(block, col_count) * tile_cols, 8), tile_cols)
                u = c_ref[cols, at][None, :, :] + r_ref[rows, at][:, None, :]
                y = x[b * tokens : (b + 1) * tokens] + u.reshape(tokens, wide)
                to = pl.ds(pl.multiple_of(block * tokens, tokens), tokens)
                for g in range(2):
                    head = start // size + g
                    z = y[:, g * size : (g + 1) * size]
                    if head < heads:
                        gain = gain_ref[:, head_width + head * size : head_width + (head + 1) * size]
                        z = normed(z, rstd[b], gain)
                    else:
                        z = z * rstd[b]
                    kv_ref[head, to, :] = z.astype(BF16)
        return carry

    lax.fori_loop(0, rounds, keys_values, 0)

    def attend(s):
        wait(qbuf_ref, q_sem)
        for start in range(0, head_width, size):
            at = slice(start, start + size)
            x = jnp.dot(qbuf_ref[...], f_ref[:, at], preferred_element_type=F32)
            for side in range(2):
                mine = q_row(s, side)
                cols = pl.ds(pl.multiple_of(lax.rem(mine, per_line) * owned, owned), owned)
                own_rows = pl.ds(pl.multiple_of(row * tile_rows, 8), tile_rows)
                u = c_ref[cols, at] + pick(r_ref[own_rows, at], lax.div(mine, per_line))
                rstd = jnp.broadcast_to(pick(rq_ref[...], mine), (size, owned)).T
                y = normed(x[side * owned : (side + 1) * owned] + u, rstd, gain_ref[:, at])
                q_ref[start // size, side * owned : (side + 1) * owned, :] = y.astype(BF16)

        @pl.when(s + 1 < lines)
        def _():
            fetch_q(s + 1)

        def one_head(h, carry):
            to = pl.ds(pl.multiple_of(h * size, size), size)
            ctx_ref[s, :, to] = attention_block(
                key_block, q_ref[h], kv_ref.at[h], kv_ref.at[heads + h]
            )
            return carry

        lax.fori_loop(0, heads, one_head, 0)

    chunk = math.gcd(part, 512)

    def project_out(n, s, j):
        slot = lax.rem(n, 2)
        dest = order(s)

        @pl.when(n >= 2)
        def _():
            wait(stage_ref.at[slot], stage_send.at[slot])

        def columns(i, carry):
            at = pl.ds(pl.multiple_of(i * chunk, chunk), chunk)
            x = jnp.dot(ctx_ref[s], wall_ref[j, :, at], preferred_element_type=F32).astype(BF16)
            stage_ref[slot, :, at] = x[:owned]
            own_ref[:, at] = x[owned:]
            return carry

        lax.fori_loop(0, part // chunk, columns, 0)
        remote(stage_ref.at[slot], pair_ref.at[dest, j], stage_send.at[slot],
               pair_recv.at[dest, j], row, partner).start()
        wait(pair_ref.at[dest, j], pair_recv.at[dest, j])
        pair_ref[dest, j] = (pair_ref[dest, j].astype(F32) + own_ref[...].astype(F32)).astype(BF16)

    def pass_on(s, j):
        dest = order(s)
        up = dest > line
        to = jnp.where(up, line + 1, line - 1)
        slot = jnp.where(jnp.logical_and(dest == to, jnp.logical_not(up)), lines, dest)

        @pl.when(jnp.logical_not(is_end))
        def _():
            wait(hop_ref.at[dest, j], hop_recv.at[dest, j])
            total = pair_ref[dest, j].astype(F32) + hop_ref[dest, j].astype(F32)
            pair_ref[dest, j] = total.astype(BF16)

        remote(pair_ref.at[dest, j], hop_ref.at[slot, j], hop_send.at[dest, j],
               hop_recv.at[slot, j], row, 2 * to + core).start()

    inner = row_count - 2

    def group_size(s):
        return jnp.where(s == 0, 1, jnp.where(s == 1, 1 + 2 * inner, 1 + inner))

    def member(s, t):
        u = t - 1
        early = jnp.logical_and(s == 1, t > 0)
        return (jnp.where(early, lax.div(u, inner), s),
                jnp.where(early, 1 + lax.rem(u, inner), t))

    def group_start(s):
        return jnp.where(s < 2, s, 2 + 2 * inner + (s - 2) * (1 + inner))

    def step(s, carry):
        attend(s)

        @pl.when(s == 1)
        def _():
            for hop in range(1, row_count - 1):
                wait(wall_ref.at[hop], w_recv.at[hop])
            if relay:
                for side in range(2):
                    relayed(side).start()

        def make(t, c):
            ss, j = member(s, t)
            project_out(group_start(s) + t, ss, j)

            @pl.when(jnp.logical_and(is_end, ss < lines - 1))
            def _():
                pass_on(ss, j)

            return c

        lax.fori_loop(0, group_size(s), make, 0)

        @pl.when(jnp.logical_and(s > 0, jnp.logical_not(is_end)))
        def _():
            def late(t, c):
                pass_on(*member(s - 1, t))
                return c

            lax.fori_loop(0, group_size(s - 1), late, 0)

        return carry

    pltpu.make_async_copy(w_ref, wall_ref.at[0], w_local).wait()
    lax.fori_loop(0, lines, step, 0)
    final = row_count - 1
    if relay:
        for side in range(2):
            relayed(side).wait_recv()
    else:
        wait(wall_ref.at[final], w_recv.at[final])

    def make_last(s, c):
        project_out(group_start(lines) + s, s, final)

        @pl.when(jnp.logical_and(is_end, s < lines - 1))
        def _():
            pass_on(s, final)

        return c

    lax.fori_loop(0, lines, make_last, 0)

    def finish(j, sender):
        to = pl.ds(pl.multiple_of(sender * part, 128), part)
        side = jnp.where(line > 0, line, lines)
        wait(hop_ref.at[side, j], hop_recv.at[side, j])

        @pl.when(is_end)
        def _():
            total = pair_ref[line, j].astype(F32) + hop_ref[side, j].astype(F32)
            out_ref[:, to] = total.astype(BF16)

        @pl.when(jnp.logical_not(is_end))
        def _():
            wait(hop_ref.at[lines, j], hop_recv.at[lines, j])
            total = pair_ref[line, j].astype(F32) + hop_ref[line, j].astype(F32)
            out_ref[:, to] = (total + hop_ref[lines, j].astype(F32)).astype(BF16)

    def sender_of(hop):
        if hop == 0:
            return row
        if row_count == 4:
            return row_peer(row, hop, row_count)
        return lax.rem(row + row_count - hop, row_count)

    for j in range(row_count - 1):
        finish(j, sender_of(j))

    @pl.when(jnp.logical_not(is_end))
    def _():
        def late(s, c):
            pass_on(s, final)
            return c

        lax.fori_loop(0, lines - 1, late, 0)

    finish(final, sender_of(final))
    for hop in range(1, 3 if relay else row_count):
        wait(w_ref, w_send.at[hop])
    if relay:
        for side in range(2):
            relayed(side).wait_send()
    for slot in range(2):
        wait(stage_ref.at[slot], stage_send.at[slot])

    def drain(s, c):
        for j in range(row_count):
            wait(pair_ref.at[order(s), j], hop_send.at[order(s), j])
        return c

    lax.fori_loop(0, lines - 1, drain, 0)


def attend(pixels, f, r, c, gain, rstd, rq, w_out, sizes, heads, size):
    row_count, col_count, tile_rows, tile_cols = sizes
    devices, tokens, pix = pixels.shape
    head_width, part = w_out.shape
    lines = col_count // 2
    owned = tile_cols * tile_rows
    count = devices * tokens
    blocks = math.gcd(devices, 4)
    vmem = lambda: pl.BlockSpec(memory_space=pltpu.VMEM)
    hbm = lambda: pl.BlockSpec(memory_space=pl.ANY)
    dma = pltpu.SemaphoreType.DMA
    return pl.pallas_call(
        functools.partial(attend_kernel, sizes, heads, math.gcd(count, KEY_BLOCK)),
        in_specs=[hbm(), vmem(), vmem(), vmem(), vmem(), vmem(), vmem(), hbm()],
        out_specs=vmem(),
        out_shape=jax.ShapeDtypeStruct((owned, part * row_count), BF16),
        scratch_shapes=[
            pltpu.VMEM((2 * heads, count, size), BF16),
            pltpu.VMEM((row_count, head_width, part), BF16),
            pltpu.VMEM((2, blocks, tokens, pix), BF16),
            pltpu.VMEM((2 * owned, pix), BF16),
            pltpu.VMEM((heads, 2 * owned, size), BF16),
            pltpu.VMEM((lines, 2 * owned, head_width), BF16),
            pltpu.VMEM((lines, row_count, owned, part), BF16),
            pltpu.VMEM((lines + 1, row_count, owned, part), BF16),
            pltpu.VMEM((owned, part), BF16),
            pltpu.VMEM((2, owned, part), BF16),
            dma,
            dma((row_count + 1,)),
            dma((row_count + 1,)),
            dma((2,)),
            dma,
            dma((2,)),
            dma((lines, row_count)),
            dma((lines, row_count)),
            dma((lines + 1, row_count)),
        ],
        compiler_params=pltpu.CompilerParams(
            vmem_limit_bytes=63 * 1024 * 1024, has_side_effects=True
        ),
        cost_estimate=pl.CostEstimate(
            flops=8 * owned * lines * count * head_width,
            bytes_accessed=4 * count * head_width,
            transcendentals=heads * owned * col_count * count,
        ),
        name="attend",
    )(pixels, f, r, c, gain, rstd, rq, w_out)


def local(patches, w_patch, patch_bias, ln_gain, w_qkv, qk_gain, w_out):
    tile_rows, tile_cols, pix = patches.shape
    model_width = w_patch.shape[1]
    heads, size = w_qkv.shape[2], w_qkv.shape[3]
    head_width = heads * size
    col_count, row_count = lax.axis_size("col"), lax.axis_size("row")
    sizes = (row_count, col_count, tile_rows, tile_cols)
    grid_rows, grid_cols = tile_rows * row_count, tile_cols * col_count
    assert grid_cols % (tile_rows * tile_cols) == 0
    bias = patch_bias.astype(F32)[None, :]
    gain = ln_gain.astype(F32)[None, :]
    table = sincos_half(jnp.arange(max(grid_rows, grid_cols), dtype=jnp.int32), model_width)
    heads_w = w_qkv.transpose(1, 2, 0, 3).reshape(3 * heads, model_width, size)
    f, r, c, pixels, rstd = prep(
        patches.reshape(-1, pix), w_patch, gain, bias, table, heads_w, sizes, heads,
        grid_rows, grid_cols
    )
    rq = rstd[:, 0, :].reshape(row_count, col_count, tile_rows, tile_cols)
    rq = lax.dynamic_index_in_dim(rq, lax.axis_index("row"), 0, keepdims=False)
    rq = rq.transpose(1, 0, 2).reshape(col_count, tile_rows * tile_cols)
    exp_factor = math.log2(math.e) / math.sqrt(size)
    gains = jnp.concatenate(
        [qk_gain[0].reshape(1, -1) * exp_factor, qk_gain[1].reshape(1, -1)], axis=1
    )
    return attend(
        pixels, f, r, c, gains, rstd, rq, w_out.reshape(head_width, -1), sizes, heads, size
    )


def solution(mesh):
    return jax.shard_map(
        local,
        mesh=mesh,
        in_specs=(
            P("row", "col", None),
            P(),
            P(),
            P(),
            P(None, None, "col", None),
            P(None, "col", None),
            P("col", None, "row"),
        ),
        out_specs=P(("row", "col"), None),
        check_vma=False,
    )
```

time: 390 us -> 244 us (0.63)
  waiting for transfers between devices: 162 us -> 0 us
  Pallas kernels: 131 us -> 233 us
  matrix products: 36.3 us -> 0 us
  blocking collectives: 22.9 us -> 0 us
  between operations: 13.7 us -> 0.06 us
  local copies, waits for them, and re-layouts: 16.2 us -> 5.16 us
    reduce_scatter x4 -> x0, waiting for transfers between devices: 102 us -> none  [local(): lax.psum_scatter(partial, 'col', scatter_dimension=0, tiled=True)]
    pallas_call x7 -> x2, Pallas kernels: 131 us -> 233 us  [the longest x1 165 us: attend(): pl.pallas_call(functools.partial(attend_kernel, sizes, heads, math.gcd(co...]
    all_gather x3 -> x0, waiting for transfers between devices: 57.9 us -> none  [the longest x1 29.7 us: local(): pixels = lax.all_gather(patches, 'col', axis=1, tiled=True)]
    dot_general x5 -> x0, matrix products: 36.3 us -> none  [the longest x4 31 us: local(): jnp.dot(context.reshape(col_count * chunk_rows, head_width), out_weight,...]
    all_gather x2 -> x0, blocking collectives: 22.9 us -> none  [the longest x1 14.1 us: local(): rstd = lax.all_gather(rstd, 'col', axis=1, tiled=True)]
    slice x6 -> x1, local copies, waits for them, and re-layouts: 6.49 us -> 0.95 us  [local(): rq = rstd[:, 0, :].reshape(row_count, col_count, tile_rows, tile_cols)]
    dynamic_slice x5 -> x2, local copies, waits for them, and re-layouts: 4.43 us -> 0.02 us  [local(): rq = lax.dynamic_index_in_dim(rq, lax.axis_index('row'), 0, keepdims=False)]
  transfers between devices with their start and end apart: 7 -> 0, of which waited for: 5 -> 0; matrix products, arithmetic and copies ran while one was open for 12% -> 0% of each run, Pallas kernels for 34% -> 0%
where the time goes in v2:
time: 244 us
  Pallas kernels  233 us (95%)
  other arithmetic  6.12 us (3%)
  local copies, waits for them, and re-layouts  5.16 us (2%)
    pallas_call x1, Pallas kernels, attend(): pl.pallas_call(functools.partial(attend_kernel, sizes, heads, math.gcd(co...  165 us
    pallas_call x1, Pallas kernels, prep(): pl.pallas_call(functools.partial(prep_kernel, sizes, group, 2 * heads_her...  67.9 us

profile of v2, /device:TPU:0, one launch (start us, length us, event | category | flops | bytes accessed | tf_op | source)
XLA Modules:
  0.0 244.1 jit_solution(4621760192354659818)
XLA Ops:
  0.0 3.0 %fusion.1 = (f32[128]{0:T(128)S(1)}, f32[128]{0:T(128)S(1)}, f32[128,1536]{1,0:T(8,128)S(1)}, f32[128,1536]{1,0:T(8,128)S(1)}) fusion(f32[1536]{0:T(1024)S(1)} %negate_power_fusion, f32[128]{0:T(128)S(1)} %iota_convert_fusion), kind=kLoop, calls=%fused_computation.4 | loop fusion | flops 589568 | bytes 1580544 | tf_op jit(solution)/shard_map/reduce_sum | solution.py:210
  3.1 0.7 copy.8.tmean_ref
  3.8 0.0 copy-start
  3.8 0.0 copy-start.1
  3.8 1.2 pad_maximum_fusion.table_ref
  5.0 0.0 copy-done
  5.1 0.6 broadcast_in_dim.17
  5.7 0.0 copy-done.1
  5.7 0.6 broadcast_in_dim.18
  6.3 0.0 copy-start.2
  6.3 67.9 %prep.1 = (bf16[768,2304]{1,0:T(8,128)(2,1)}, f32[32,2304]{1,0:T(8,128)}, f32[128,2304]{1,0:T(8,128)}, bf16[32,128,768]{2,1,0:T(8,128)(2,1)}, f32[32,8,128]{2,1,0:T(8,128)}) custom-call(bf16[128,768]{1,0:T(8,128)(2,1)} %bitcast.23, bf16[768,6144]{1,0:T(8,128)(2,1)} %wp_ref.1, f32[1,6144]{1,0:T(1,128)} %bitcast.19, f32[1,6144]{1,0:T(1,128)} %bitcast.20, ...), custom_call_target="tpu_custom_call" | custom-call | flops 25820135424 | bytes 28311552 | tf_op jit(solution)/shard_map/prep/pallas_call | solution.py:212
  74.1 0.9 slice_reduce_fusion
  75.1 0.1 reshape_squeeze.8
  75.2 0.7 reshape.56.rq_ref
  75.9 0.0 copy-done.2
  75.9 0.6 pad_maximum_fusion.1.gain_ref
  76.5 164.8 %attend.1 = bf16[128,6144]{1,0:T(8,128)(2,1)} custom-call(bf16[32,128,768]{2,1,0:T(8,128)(2,1)} %get-tuple-element.10.pixels_ref, bf16[768,2304]{1,0:T(8,128)(2,1)} %get-tuple-element.11.f_ref, f32[32,2304]{1,0:T(8,128)} %get-tuple-element.12.r_ref, f32[128,2304]{1,0:T(8,128)} %get-tuple-element.13.c_ref, f32[1,1536]{1,0:T(1,128)} %pad_maximum_fusion.1.gain_ref, ...), custom_call_target="tpu_custom_call" | custom-call | flops 12884901888 | bytes 12582912 | tf_op jit(solution)/shard_map/attend/pallas_call | solution.py:587
  241.4 2.7 %copy.13 = bf16[128,6144]{1,0:T(8,128)(2,1)} copy(bf16[128,6144]{1,0:T(8,128)(2,1)} %attend.1) | data formatting | bytes 3145728
  (6 shorter events, 0.0 us)
Async XLA Ops:
  3.8 1.3 copy-start
  3.8 1.9 copy-start.1
  6.3 69.6 %copy-start.2 = (f32[2,6,128]{2,0,1:T(2,128)S(1)}, f32[2,6,128]{2,0,1:T(2,128)}, u32[]{:S(2)}) copy-start(f32[2,6,128]{2,0,1:T(2,128)} %param.12) | copy-start | bytes 18436

commit v3 on v2

--- a/solution.py
+++ b/solution.py
@@ -10,7 +10,6 @@
 
 NORM_EPS = 1e-06
 KEY_BLOCK = 1024
-CHUNKS = 4
 MISC = 16
 F32 = jnp.float32
 BF16 = jnp.bfloat16
@@ -46,9 +45,9 @@
 
 
 def prep_kernel(sizes, group, centred_steps, patch_ref, wp_ref, gain_ref, bias_ref, table_ref,
-                tmean_ref, w_ref, f_ref, r_ref, c_ref, pixels_ref, rstd_ref,
-                a_ref, acc_ref, row_acc, e_ref, mine_ref, seen_ref,
-                local_sem, send_sem, recv_sem, stat_send, stat_recv):
+                w_ref, wout_ref, f_ref, r_ref, c_ref, pixels_ref, rstd_ref, early_ref,
+                a_ref, acc_ref, row_acc, e_ref, mean_ref, tmean_ref, mine_ref, seen_ref, held_ref,
+                save_sem, send_sem, recv_sem, stat_send, stat_recv, early_send, early_recv):
     row_count, col_count, tile_rows, tile_cols = sizes
     step = pl.program_id(0)
     last = pl.num_programs(0) - 1
@@ -64,14 +63,29 @@
     lines = col_count // 2
     partner = 2 * line + 1 - core
 
+    relay = row_count == 4
+    near = (1, 2) if relay else tuple(range(1, row_count))
+
+    def early(side, portion):
+        tall, piece = early_ref.shape[1] // 2, early_ref.shape[2]
+        rows = pl.ds(portion * tall, tall)
+        at = 2 * side + portion
+        return remote(wout_ref.at[rows, pl.ds(side * piece, piece)], early_ref.at[side, rows],
+                      early_send.at[at], early_recv.at[at],
+                      row_peer(row, 1 + side, row_count), col)
+
     def give(src, block, to_row, to_col):
-        remote(src, pixels_ref.at[block], send_sem, recv_sem.at[block], to_row, to_col).start()
+        remote(src, held_ref.at[block], send_sem, recv_sem.at[block], to_row, to_col).start()
+
+    def save(block):
+        pltpu.make_async_copy(held_ref.at[block], pixels_ref.at[block], save_sem).start()
 
     def got(block):
-        pltpu.make_async_copy(pixels_ref.at[block], pixels_ref.at[block], recv_sem.at[block]).wait()
+        pltpu.make_async_copy(held_ref.at[block], held_ref.at[block], recv_sem.at[block]).wait()
+        save(block)
 
     def to_rows(src, block):
-        for hop in range(1, row_count):
+        for hop in near:
             give(src, block, row_peer(row, hop, row_count), col)
 
     @pl.when(step == 0)
@@ -80,14 +94,27 @@
             give(patch_ref, me, row, 2 * lax.rem(line + hop, lines) + core)
         to_rows(patch_ref, me)
         give(patch_ref, me, row, partner)
-        pltpu.make_async_copy(patch_ref, pixels_ref.at[me], local_sem).start()
+        pltpu.make_async_copy(patch_ref, pixels_ref.at[me], save_sem).start()
+        if relay:
+            for side in range(2):
+                early(side, 0).start()
         gain = gain_ref[...]
+
+        ones = jnp.ones((width, 128), BF16)
+        tall = math.gcd(pix, 128)
+
+        def average(i, carry):
+            rows = pl.ds(pl.multiple_of(i * tall, tall), tall)
+            total = jnp.dot(wp_ref[rows, :], ones, preferred_element_type=F32)
+            mean_ref[rows, :] = total * (1.0 / width)
+            return carry
+
+        lax.fori_loop(0, pix // tall, average, 0)
 
         def centre(i, carry):
             rows = pl.ds(pl.multiple_of(i * 16, 16), 16)
             w = wp_ref[rows, :].astype(F32)
-            mean = jnp.sum(w, axis=1, keepdims=True) * (1.0 / width)
-            a_ref[rows, :] = ((w - mean) * gain).astype(BF16)
+            a_ref[rows, :] = ((w - mean_ref[rows, 0:1]) * gain).astype(BF16)
             return carry
 
         lax.fori_loop(0, pix // 16, centre, 0)
@@ -102,6 +129,9 @@
             rows = pl.ds(pl.multiple_of(i * 16, 16), 16)
             to = pl.ds(pl.multiple_of(base + i * 16, 16), 16)
             t = table_ref[rows, :]
+            tmean_ref[rows, :] = jnp.broadcast_to(
+                jnp.sum(t, axis=1, keepdims=True) * (1.0 / width), (16, 128)
+            )
             a_ref[to, :half] = (t * gain[:, :half]).astype(BF16)
             a_ref[to, half:] = (t * gain[:, half:]).astype(BF16)
             return carry
@@ -124,13 +154,26 @@
                 else:
                     t = jnp.broadcast_to(table_ref[own_cols, at][None, :, :], shape)
                 e = jnp.dot(patch_ref[...], wp_ref[:, to], preferred_element_type=F32)
-                e_ref[:, to] = e + bias_ref[:, to] + t.reshape(tokens, chunk)
-            return carry
-
-        lax.fori_loop(0, half // chunk, embed, 0)
-        mean = jnp.sum(e_ref[...], axis=1, keepdims=True) * (1.0 / width)
-        centred = e_ref[...] - mean
-        variance = jnp.sum(centred * centred, axis=1, keepdims=True) * (1.0 / width)
+                e = e + bias_ref[:, to] + t.reshape(tokens, chunk)
+                e_ref[:, to] = e
+                for start in range(0, chunk, 128):
+                    carry = carry + e[:, start : start + 128]
+            return carry
+
+        zero = jnp.zeros((tokens, 128), F32)
+        total = lax.fori_loop(0, half // chunk, embed, zero)
+        mean = jnp.sum(total, axis=1, keepdims=True) * (1.0 / width)
+
+        def spread(i, carry):
+            at = pl.ds(pl.multiple_of(i * chunk, chunk), chunk)
+            e = e_ref[:, at] - mean
+            for start in range(0, chunk, 128):
+                part = e[:, start : start + 128]
+                carry = carry + part * part
+            return carry
+
+        total = lax.fori_loop(0, width // chunk, spread, zero)
+        variance = jnp.sum(total, axis=1, keepdims=True) * (1.0 / width)
         rstd = jnp.broadcast_to(lax.rsqrt(variance + NORM_EPS), (tokens, 128))
         mine_ref[...] = rstd.T[:8, :]
 
@@ -143,13 +186,26 @@
         lax.fori_loop(1, devices, tell, 0)
         seen_ref[devices - 1] = mine_ref[...]
 
-    @pl.when(step == jnp.minimum(3, last))
+    @pl.when(step == jnp.minimum(2, last))
     def _():
         for hop in range(1, lines):
             block = row * col_count + 2 * lax.rem(line + hop, lines) + core
             got(block)
-            to_rows(pixels_ref.at[block], block)
-            give(pixels_ref.at[block], block, row, partner)
+            to_rows(held_ref.at[block], block)
+            give(held_ref.at[block], block, row, partner)
+
+    if relay:
+        @pl.when(step == jnp.minimum(6, last))
+        def _():
+            for i in range(lines):
+                for hop in (1, 2):
+                    block = row_peer(row, hop, row_count) * col_count + 2 * i + core
+                    got(block)
+                    if (2 * i < lines) == (hop == 1):
+                        give(held_ref.at[block], block, row_peer(row, 3 - hop, row_count), col)
+                    give(held_ref.at[block], block, row, partner)
+            for side in range(2):
+                early(side, 1).start()
 
     def product(start):
         ks = slice(start, start + half)
@@ -162,8 +218,8 @@
     acc_ref[...] += product(half)
     bias_w = acc_ref[pix : pix + 1, :] + acc_ref[pix + 1 : pix + 2, :]
     gain_w = acc_ref[pix + 2 : pix + 3, :]
-    r = row_acc[...] - tmean_ref[:grid_rows, :] * gain_w
-    c = acc_ref[base : base + grid_cols, :] - tmean_ref[:grid_cols, :] * gain_w + bias_w
+    r = row_acc[...] - tmean_ref[:grid_rows, 0:1] * gain_w
+    c = acc_ref[base : base + grid_cols, :] - tmean_ref[:grid_cols, 0:1] * gain_w + bias_w
     f = acc_ref[:pix, :]
     size = f.shape[1] // group
     keep = jnp.where(step < centred_steps, 1.0, 0.0).astype(F32)
@@ -176,17 +232,16 @@
 
     @pl.when(step == last)
     def _():
-        for hop in range(1, row_count):
+        for hop in (3,) if relay else near:
             for i in range(lines):
                 block = row_peer(row, hop, row_count) * col_count + 2 * i + core
                 got(block)
-                give(pixels_ref.at[block], block, row, partner)
+                give(held_ref.at[block], block, row, partner)
         for other in range(row_count):
             for i in range(lines):
                 got(other * col_count + 2 * i + 1 - core)
-        everyone = pixels_ref.at[pl.ds(0, devices - 1)]
+        everyone = held_ref.at[pl.ds(0, devices - 1)]
         pltpu.make_async_copy(everyone, everyone, send_sem).wait()
-        pltpu.make_async_copy(patch_ref, pixels_ref.at[me], local_sem).wait()
         seen = seen_ref.at[pl.ds(0, devices - 1)]
         pltpu.make_async_copy(seen, seen, stat_recv).wait()
         pltpu.make_async_copy(seen, seen, stat_send).wait()
@@ -196,9 +251,14 @@
             return carry
 
         lax.fori_loop(0, devices, put, 0)
-
-
-def prep(patches, w_patch, gain, bias, table, heads_w, sizes, heads_here, grid_rows, grid_cols):
+        pltpu.make_async_copy(pixels_ref, pixels_ref, save_sem).wait()
+        if relay:
+            for side in range(2):
+                early(side, 0).wait()
+                early(side, 1).wait()
+
+
+def prep(patches, w_patch, gain, bias, table, heads_w, w_out, sizes, heads_here, grid_rows, grid_cols):
     pix, width = w_patch.shape
     total, _, size = heads_w.shape
     group = next(g for g in (2, 3, 1) if heads_here % g == 0)
@@ -207,7 +267,6 @@
     rows = pix + MISC + positions
     tokens = patches.shape[0]
     devices = sizes[0] * sizes[1]
-    tmean = jnp.sum(table, axis=1, keepdims=True) / width
     whole = lambda s: pl.BlockSpec(s, lambda i: (0,) * len(s), pipeline_mode=pl.Buffered(1))
     return pl.pallas_call(
         functools.partial(prep_kernel, sizes, group, 2 * heads_here // group),
@@ -218,8 +277,8 @@
             whole((1, width)),
             whole((1, width)),
             whole(table.shape),
-            whole((positions, 1)),
             pl.BlockSpec((group, width, size), lambda i: (i, 0, 0)),
+            pl.BlockSpec(memory_space=pl.ANY),
         ],
         out_specs=[
             pl.BlockSpec((pix, group * size), lambda i: (0, i)),
@@ -227,6 +286,7 @@
             pl.BlockSpec((grid_cols, group * size), lambda i: (0, i)),
             pl.BlockSpec(memory_space=pl.ANY),
             pl.BlockSpec((devices, 8, tokens), lambda i: (0, 0, 0)),
+            pl.BlockSpec(memory_space=pl.ANY),
         ],
         out_shape=[
             jax.ShapeDtypeStruct((pix, total * size), BF16),
@@ -234,19 +294,25 @@
             jax.ShapeDtypeStruct((grid_cols, total * size), F32),
             jax.ShapeDtypeStruct((devices, tokens, pix), BF16),
             jax.ShapeDtypeStruct((devices, 8, tokens), F32),
+            jax.ShapeDtypeStruct((2, w_out.shape[0], w_out.shape[1] // 2), BF16),
         ],
         scratch_shapes=[
             pltpu.VMEM((rows, width), BF16),
             pltpu.VMEM((rows, group * size), F32),
             pltpu.VMEM((grid_rows, group * size), F32),
             pltpu.VMEM((tokens, width), F32),
+            pltpu.VMEM((pix, 128), F32),
+            pltpu.VMEM((positions, 128), F32),
             pltpu.VMEM((8, tokens), F32),
             pltpu.VMEM((devices, 8, tokens), F32),
+            pltpu.VMEM((devices, tokens, pix), BF16),
             pltpu.SemaphoreType.DMA,
             pltpu.SemaphoreType.DMA,
             pltpu.SemaphoreType.DMA((devices,)),
             pltpu.SemaphoreType.DMA,
             pltpu.SemaphoreType.DMA,
+            pltpu.SemaphoreType.DMA((4,)),
+            pltpu.SemaphoreType.DMA((4,)),
         ],
         compiler_params=pltpu.CompilerParams(
             dimension_semantics=("arbitrary",), vmem_limit_bytes=60 * 1024 * 1024,
@@ -258,7 +324,7 @@
             transcendentals=0,
         ),
         name="prep",
-    )(patches, w_patch, gain, bias, table, tmean, heads_w)
+    )(patches, w_patch, gain, bias, table, heads_w, w_out)
 
 def attention_block(key_block, query, k_ref, v_ref):
     rows, head_size = query.shape
@@ -284,8 +350,8 @@
 
 
 def attend_kernel(sizes, heads, key_block, pixels_ref, f_ref, r_ref, c_ref, gain_ref, rstd_ref,
-                  rq_ref, w_ref, out_ref, kv_ref, wall_ref, pbuf_ref, qbuf_ref, q_ref, ctx_ref,
-                  pair_ref, hop_ref, own_ref, stage_ref, w_local, w_send, w_recv, p_sem, q_sem,
+                  rq_ref, w_ref, early_ref, out_ref, kv_ref, wall_ref, pbuf_ref, qbuf_ref, q_ref, ctx_ref,
+                  pair_ref, hop_ref, own_ref, stage_ref, w_local, early_sem, w_send, w_recv, p_sem, q_sem,
                   stage_send, pair_recv, hop_send, hop_recv):
     row_count, col_count, tile_rows, tile_cols = sizes
     row, col, line, core = ids()
@@ -298,6 +364,7 @@
     per_line = tile_cols * col_count // owned
     part = wall_ref.shape[2]
     wide = 2 * size
+    exp_factor = math.log2(math.e) / math.sqrt(size)
     is_end = jnp.logical_or(line == 0, line == lines - 1)
 
     def wait(ref, sem):
@@ -312,15 +379,29 @@
     relay = row_count == 4
     piece = part // 2
 
+    def half(side):
+        return pl.ds(side * piece, piece)
+
+    def load_early(side):
+        return pltpu.make_async_copy(
+            early_ref.at[side], wall_ref.at[1 + side, :, half(side)], early_sem.at[side]
+        )
+
+    def rest(side):
+        at = half(1 - side)
+        return remote(wall_ref.at[0, :, at], wall_ref.at[1 + side, :, at], w_send.at[1 + side],
+                      w_recv.at[1 + side], row_peer(row, 1 + side, row_count), col)
+
     def relayed(side):
-        at = pl.ds(side * piece, piece)
+        at = half(side)
         return remote(wall_ref.at[1 + side, :, at], wall_ref.at[3, :, at], w_send.at[3 + side],
                       w_recv.at[3 + side], row_peer(row, 2 - side, row_count), col)
 
-    for hop in range(1, 3 if relay else row_count):
-        remote(w_ref, wall_ref.at[hop], w_send.at[hop], w_recv.at[hop],
-               row_peer(row, hop, row_count), col).start()
-    pltpu.make_async_copy(w_ref, wall_ref.at[0], w_local).start()
+    fetch_w = pltpu.make_async_copy(w_ref, wall_ref.at[0], w_local)
+    fetch_w.start()
+    if relay:
+        load_early(0).start()
+        load_early(1).start()
 
     def fetch(i):
         slot = lax.rem(i, 2)
@@ -353,6 +434,17 @@
 
     fetch(0).start()
     fetch_q(0)
+    fetch_w.wait()
+    if relay:
+        for side in range(2):
+            rest(side).start()
+        for side in range(2):
+            load_early(side).wait()
+            relayed(side).start()
+    else:
+        for hop in range(1, row_count):
+            remote(wall_ref.at[0], wall_ref.at[hop], w_send.at[hop], w_recv.at[hop],
+                   row_peer(row, hop, row_count), col).start()
     rounds = pixels_ref.shape[0] // blocks
 
     def keys_values(i, carry):
@@ -381,7 +473,7 @@
                     head = start // size + g
                     z = y[:, g * size : (g + 1) * size]
                     if head < heads:
-                        gain = gain_ref[:, head_width + head * size : head_width + (head + 1) * size]
+                        gain = gain_ref[1:2, head * size : (head + 1) * size]
                         z = normed(z, rstd[b], gain)
                     else:
                         z = z * rstd[b]
@@ -392,17 +484,25 @@
 
     def attend(s):
         wait(qbuf_ref, q_sem)
-        for start in range(0, head_width, size):
-            at = slice(start, start + size)
-            x = jnp.dot(qbuf_ref[...], f_ref[:, at], preferred_element_type=F32)
-            for side in range(2):
-                mine = q_row(s, side)
-                cols = pl.ds(pl.multiple_of(lax.rem(mine, per_line) * owned, owned), owned)
-                own_rows = pl.ds(pl.multiple_of(row * tile_rows, 8), tile_rows)
-                u = c_ref[cols, at] + pick(r_ref[own_rows, at], lax.div(mine, per_line))
-                rstd = jnp.broadcast_to(pick(rq_ref[...], mine), (size, owned)).T
-                y = normed(x[side * owned : (side + 1) * owned] + u, rstd, gain_ref[:, at])
-                q_ref[start // size, side * owned : (side + 1) * owned, :] = y.astype(BF16)
+        own_rows = pl.ds(pl.multiple_of(row * tile_rows, 8), tile_rows)
+        sides = []
+        for side in range(2):
+            mine = q_row(s, side)
+            cols = pl.ds(pl.multiple_of(lax.rem(mine, per_line) * owned, owned), owned)
+            rstd = jnp.broadcast_to(pick(rq_ref[...], mine), (size, owned)).T
+            sides.append((lax.div(mine, per_line), cols, rstd))
+        step_width = wide if head_width % wide == 0 else size
+        for start in range(0, head_width, step_width):
+            span = slice(start, start + step_width)
+            x = jnp.dot(qbuf_ref[...], f_ref[:, span], preferred_element_type=F32)
+            for g in range(step_width // size):
+                at = slice(start + g * size, start + (g + 1) * size)
+                for side, (line_row, cols, rstd) in enumerate(sides):
+                    rows = slice(side * owned, (side + 1) * owned)
+                    y = x[rows, g * size : (g + 1) * size]
+                    y = y + (c_ref[cols, at] + pick(r_ref[own_rows, at], line_row))
+                    y = normed(y, rstd, gain_ref[0:1, at] * exp_factor)
+                    q_ref[start // size + g, rows, :] = y.astype(BF16)
 
         @pl.when(s + 1 < lines)
         def _():
@@ -431,14 +531,22 @@
             at = pl.ds(pl.multiple_of(i * chunk, chunk), chunk)
             x = jnp.dot(ctx_ref[s], wall_ref[j, :, at], preferred_element_type=F32).astype(BF16)
             stage_ref[slot, :, at] = x[:owned]
-            own_ref[:, at] = x[owned:]
+            own_ref[slot, :, at] = x[owned:]
             return carry
 
         lax.fori_loop(0, part // chunk, columns, 0)
         remote(stage_ref.at[slot], pair_ref.at[dest, j], stage_send.at[slot],
                pair_recv.at[dest, j], row, partner).start()
+
+    def settle(n, s, j):
+        dest = order(s)
+        own = own_ref[lax.rem(n, 2)].astype(F32)
         wait(pair_ref.at[dest, j], pair_recv.at[dest, j])
-        pair_ref[dest, j] = (pair_ref[dest, j].astype(F32) + own_ref[...].astype(F32)).astype(BF16)
+        pair_ref[dest, j] = (pair_ref[dest, j].astype(F32) + own).astype(BF16)
+
+        @pl.when(jnp.logical_and(is_end, s < lines - 1))
+        def _():
+            pass_on(s, j)
 
     def pass_on(s, j):
         dest = order(s)
@@ -455,54 +563,45 @@
         remote(pair_ref.at[dest, j], hop_ref.at[slot, j], hop_send.at[dest, j],
                hop_recv.at[slot, j], row, 2 * to + core).start()
 
-    inner = row_count - 2
-
-    def group_size(s):
-        return jnp.where(s == 0, 1, jnp.where(s == 1, 1 + 2 * inner, 1 + inner))
-
-    def member(s, t):
-        u = t - 1
-        early = jnp.logical_and(s == 1, t > 0)
-        return (jnp.where(early, lax.div(u, inner), s),
-                jnp.where(early, 1 + lax.rem(u, inner), t))
+    inner = row_count - 1
 
     def group_start(s):
-        return jnp.where(s < 2, s, 2 + 2 * inner + (s - 2) * (1 + inner))
+        return s * inner
 
     def step(s, carry):
         attend(s)
 
-        @pl.when(s == 1)
-        def _():
-            for hop in range(1, row_count - 1):
-                wait(wall_ref.at[hop], w_recv.at[hop])
+        @pl.when(s == 0)
+        def _():
             if relay:
                 for side in range(2):
-                    relayed(side).start()
+                    rest(side).wait_recv()
+            else:
+                for hop in range(1, row_count - 1):
+                    wait(wall_ref.at[hop], w_recv.at[hop])
 
         def make(t, c):
-            ss, j = member(s, t)
-            project_out(group_start(s) + t, ss, j)
-
-            @pl.when(jnp.logical_and(is_end, ss < lines - 1))
+            project_out(group_start(s) + t, s, t)
+
+            @pl.when(t > 0)
             def _():
-                pass_on(ss, j)
+                settle(group_start(s) + t - 1, s, t - 1)
 
             return c
 
-        lax.fori_loop(0, group_size(s), make, 0)
+        lax.fori_loop(0, inner, make, 0)
+        settle(group_start(s) + inner - 1, s, inner - 1)
 
         @pl.when(jnp.logical_and(s > 0, jnp.logical_not(is_end)))
         def _():
             def late(t, c):
-                pass_on(*member(s - 1, t))
+                pass_on(s - 1, t)
                 return c
 
-            lax.fori_loop(0, group_size(s - 1), late, 0)
+            lax.fori_loop(0, inner, late, 0)
 
         return carry
 
-    pltpu.make_async_copy(w_ref, wall_ref.at[0], w_local).wait()
     lax.fori_loop(0, lines, step, 0)
     final = row_count - 1
     if relay:
@@ -514,13 +613,14 @@
     def make_last(s, c):
         project_out(group_start(lines) + s, s, final)
 
-        @pl.when(jnp.logical_and(is_end, s < lines - 1))
-        def _():
-            pass_on(s, final)
+        @pl.when(s > 0)
+        def _():
+            settle(group_start(lines) + s - 1, s - 1, final)
 
         return c
 
     lax.fori_loop(0, lines, make_last, 0)
+    settle(group_start(lines) + lines - 1, lines - 1, final)
 
     def finish(j, sender):
         to = pl.ds(pl.multiple_of(sender * part, 128), part)
@@ -557,11 +657,13 @@
         lax.fori_loop(0, lines - 1, late, 0)
 
     finish(final, sender_of(final))
-    for hop in range(1, 3 if relay else row_count):
-        wait(w_ref, w_send.at[hop])
     if relay:
         for side in range(2):
+            rest(side).wait_send()
             relayed(side).wait_send()
+    else:
+        for hop in range(1, row_count):
+            wait(wall_ref.at[0], w_send.at[hop])
     for slot in range(2):
         wait(stage_ref.at[slot], stage_send.at[slot])
 
@@ -573,7 +675,7 @@
     lax.fori_loop(0, lines - 1, drain, 0)
 
 
-def attend(pixels, f, r, c, gain, rstd, rq, w_out, sizes, heads, size):
+def attend(pixels, f, r, c, gain, rstd, rq, w_out, early, sizes, heads, size):
     row_count, col_count, tile_rows, tile_cols = sizes
     devices, tokens, pix = pixels.shape
     head_width, part = w_out.shape
@@ -586,7 +688,7 @@
     dma = pltpu.SemaphoreType.DMA
     return pl.pallas_call(
         functools.partial(attend_kernel, sizes, heads, math.gcd(count, KEY_BLOCK)),
-        in_specs=[hbm(), vmem(), vmem(), vmem(), vmem(), vmem(), vmem(), hbm()],
+        in_specs=[hbm(), vmem(), vmem(), vmem(), vmem(), vmem(), vmem(), hbm(), hbm()],
         out_specs=vmem(),
         out_shape=jax.ShapeDtypeStruct((owned, part * row_count), BF16),
         scratch_shapes=[
@@ -598,9 +700,10 @@
             pltpu.VMEM((lines, 2 * owned, head_width), BF16),
             pltpu.VMEM((lines, row_count, owned, part), BF16),
             pltpu.VMEM((lines + 1, row_count, owned, part), BF16),
-            pltpu.VMEM((owned, part), BF16),
+            pltpu.VMEM((2, owned, part), BF16),
             pltpu.VMEM((2, owned, part), BF16),
             dma,
+            dma((2,)),
             dma((row_count + 1,)),
             dma((row_count + 1,)),
             dma((2,)),
@@ -619,7 +722,7 @@
             transcendentals=heads * owned * col_count * count,
         ),
         name="attend",
-    )(pixels, f, r, c, gain, rstd, rq, w_out)
+    )(pixels, f, r, c, gain, rstd, rq, w_out, early)
 
 
 def local(patches, w_patch, patch_bias, ln_gain, w_qkv, qk_gain, w_out):
@@ -635,19 +738,17 @@
     gain = ln_gain.astype(F32)[None, :]
     table = sincos_half(jnp.arange(max(grid_rows, grid_cols), dtype=jnp.int32), model_width)
     heads_w = w_qkv.transpose(1, 2, 0, 3).reshape(3 * heads, model_width, size)
-    f, r, c, pixels, rstd = prep(
-        patches.reshape(-1, pix), w_patch, gain, bias, table, heads_w, sizes, heads,
+    out_rows = w_out.reshape(head_width, -1)
+    f, r, c, pixels, rstd, early = prep(
+        patches.reshape(-1, pix), w_patch, gain, bias, table, heads_w, out_rows, sizes, heads,
         grid_rows, grid_cols
     )
     rq = rstd[:, 0, :].reshape(row_count, col_count, tile_rows, tile_cols)
     rq = lax.dynamic_index_in_dim(rq, lax.axis_index("row"), 0, keepdims=False)
     rq = rq.transpose(1, 0, 2).reshape(col_count, tile_rows * tile_cols)
-    exp_factor = math.log2(math.e) / math.sqrt(size)
-    gains = jnp.concatenate(
-        [qk_gain[0].reshape(1, -1) * exp_factor, qk_gain[1].reshape(1, -1)], axis=1
-    )
+    gains = qk_gain.reshape(2, head_width)
     return attend(
-        pixels, f, r, c, gains, rstd, rq, w_out.reshape(head_width, -1), sizes, heads, size
+        pixels, f, r, c, gains, rstd, rq, out_rows, early, sizes, heads, size
     )
 
 

time: 244 us -> 233 us (0.955)
  Pallas kernels: 233 us -> 223 us
    pallas_call x1, Pallas kernels: 165 us -> 151 us  [attend(): pl.pallas_call(functools.partial(attend_kernel, sizes, heads, math.gcd(co...]
    pallas_call x1, Pallas kernels: 67.9 us -> 72.1 us  [prep(): pl.pallas_call(functools.partial(prep_kernel, sizes, group, 2 * heads_her...]
    reduce_sum x1 -> x0, other arithmetic: 3.03 us -> none  [prep(): tmean = jnp.sum(table, axis=1, keepdims=True) / width]
    sin x0 -> x1, other arithmetic: none -> 2.79 us  [sincos_half(): return jnp.concatenate([jnp.sin(angle), jnp.cos(angle)], axis=1)]
where the time goes in v3:
time: 233 us
  Pallas kernels  223 us (96%)
  other arithmetic  5.26 us (2%)
  local copies, waits for them, and re-layouts  4.43 us (2%)
    pallas_call x1, Pallas kernels, attend(): pl.pallas_call(functools.partial(attend_kernel, sizes, heads, math.gcd(co...  151 us
    pallas_call x1, Pallas kernels, prep(): pl.pallas_call(functools.partial(prep_kernel, sizes, group, 2 * heads_her...  72.1 us

profile of v3, /device:TPU:0, one launch (start us, length us, event | category | flops | bytes accessed | tf_op | source)
XLA Modules:
  0.0 232.9 jit_solution(15476550836443833762)
XLA Ops:
  0.0 2.8 %multiply_sine_fusion = (f32[128,1536]{1,0:T(8,128)S(1)}, f32[128,1536]{1,0:T(8,128)S(1)}) fusion(f32[1536]{0:T(1024)S(1)} %negate_power_fusion, f32[128]{0:T(128)S(1)} %iota_convert_fusion), kind=kLoop, calls=%fused_computation.2 | loop fusion | flops 196608 | bytes 1579520 | tf_op jit(solution)/shard_map/sin | solution.py:22
  2.8 0.0 copy-start
  2.8 0.0 copy-start.1
  2.8 1.3 pad_maximum_fusion.table_ref
  4.1 0.0 copy-done
  4.1 0.6 broadcast_in_dim.16
  4.7 0.0 copy-done.1
  4.7 0.6 broadcast_in_dim.17
  5.3 72.1 %prep.1 = (bf16[768,2304]{1,0:T(8,128)(2,1)}, f32[32,2304]{1,0:T(8,128)}, f32[128,2304]{1,0:T(8,128)}, bf16[32,128,768]{2,1,0:T(8,128)(2,1)}, f32[32,8,128]{2,1,0:T(8,128)}, /*index=5*/bf16[2,768,768]{2,1,0:T(8,128)(2,1)}) custom-call(bf16[128,768]{1,0:T(8,128)(2,1)} %bitcast.19, bf16[768,6144]{1,0:T(8,128)(2,1)} %wp_ref.1, f32[1,6144]{1,0:T(1,128)} %bitcast.14, ...), custom_call_target="tpu_custom_call" | custom-call | flops 25820135424 | bytes 28311552 | tf_op jit(solution)/shard_map/prep/pallas_call | solution.py:271
  77.4 0.9 slice_reduce_fusion
  78.4 0.1 reshape_squeeze.3
  78.5 0.7 reshape.29.rq_ref
  79.2 151.0 %attend.1 = bf16[128,6144]{1,0:T(8,128)(2,1)} custom-call(bf16[32,128,768]{2,1,0:T(8,128)(2,1)} %get-tuple-element.11.pixels_ref, bf16[768,2304]{1,0:T(8,128)(2,1)} %get-tuple-element.12.f_ref, f32[32,2304]{1,0:T(8,128)} %get-tuple-element.13.r_ref, f32[128,2304]{1,0:T(8,128)} %get-tuple-element.14.c_ref, f32[2,768]{1,0:T(2,128)} %bitcast.20, ...), custom_call_target="tpu_custom_call" | custom-call | flops 12884901888 | bytes 12582912 | tf_op jit(solution)/shard_map/attend/pallas_call | solution.py:689
  230.2 2.7 %copy.15 = bf16[128,6144]{1,0:T(8,128)(2,1)} copy(bf16[128,6144]{1,0:T(8,128)(2,1)} %attend.1) | data formatting | bytes 3145728
  (4 shorter events, 0.0 us)
Async XLA Ops:
  2.8 1.3 copy-start
  2.8 1.9 copy-start.1

commit v4 on v3

--- a/solution.py
+++ b/solution.py
@@ -138,7 +138,7 @@
 
         lax.fori_loop(0, positions // 16, place, 0)
 
-    @pl.when(step == 1)
+    @pl.when(step == jnp.minimum(3, last))
     def _():
         chunk = math.gcd(half, 512)
         own_rows = pl.ds(pl.multiple_of(row * tile_rows, 8), tile_rows)
@@ -195,7 +195,7 @@
             give(held_ref.at[block], block, row, partner)
 
     if relay:
-        @pl.when(step == jnp.minimum(6, last))
+        @pl.when(step == jnp.minimum(5, last))
         def _():
             for i in range(lines):
                 for hop in (1, 2):

time: 233 us -> 231 us (level)
    pallas_call x1, Pallas kernels: 72.1 us -> 69.4 us  [prep(): pl.pallas_call(functools.partial(prep_kernel, sizes, group, 2 * heads_her...]
where the time goes in v4:
time: 231 us
  Pallas kernels  221 us (96%)
  other arithmetic  5.26 us (2%)
  local copies, waits for them, and re-layouts  4.43 us (2%)
    pallas_call x1, Pallas kernels, attend(): pl.pallas_call(functools.partial(attend_kernel, sizes, heads, math.gcd(co...  151 us
    pallas_call x1, Pallas kernels, prep(): pl.pallas_call(functools.partial(prep_kernel, sizes, group, 2 * heads_her...  69.4 us

profile of v4, /device:TPU:0, one launch (start us, length us, event | category | flops | bytes accessed | tf_op | source)
XLA Modules:
  0.0 230.5 jit_solution(16551658194370592792)
XLA Ops:
  0.0 2.8 %multiply_sine_fusion = (f32[128,1536]{1,0:T(8,128)S(1)}, f32[128,1536]{1,0:T(8,128)S(1)}) fusion(f32[1536]{0:T(1024)S(1)} %negate_power_fusion, f32[128]{0:T(128)S(1)} %iota_convert_fusion), kind=kLoop, calls=%fused_computation.2 | loop fusion | flops 196608 | bytes 1579520 | tf_op jit(solution)/shard_map/sin | solution.py:22
  2.8 0.0 copy-start
  2.8 0.0 copy-start.1
  2.8 1.3 pad_maximum_fusion.table_ref
  4.1 0.0 copy-done
  4.1 0.6 broadcast_in_dim.16
  4.7 0.0 copy-done.1
  4.7 0.6 broadcast_in_dim.17
  5.3 69.4 %prep.1 = (bf16[768,2304]{1,0:T(8,128)(2,1)}, f32[32,2304]{1,0:T(8,128)}, f32[128,2304]{1,0:T(8,128)}, bf16[32,128,768]{2,1,0:T(8,128)(2,1)}, f32[32,8,128]{2,1,0:T(8,128)}, /*index=5*/bf16[2,768,768]{2,1,0:T(8,128)(2,1)}) custom-call(bf16[128,768]{1,0:T(8,128)(2,1)} %bitcast.19, bf16[768,6144]{1,0:T(8,128)(2,1)} %wp_ref.1, f32[1,6144]{1,0:T(1,128)} %bitcast.14, ...), custom_call_target="tpu_custom_call" | custom-call | flops 25820135424 | bytes 28311552 | tf_op jit(solution)/shard_map/prep/pallas_call | solution.py:271
  74.7 0.9 slice_reduce_fusion
  75.7 0.1 reshape_squeeze.3
  75.8 0.7 reshape.29.rq_ref
  76.5 151.3 %attend.1 = bf16[128,6144]{1,0:T(8,128)(2,1)} custom-call(bf16[32,128,768]{2,1,0:T(8,128)(2,1)} %get-tuple-element.11.pixels_ref, bf16[768,2304]{1,0:T(8,128)(2,1)} %get-tuple-element.12.f_ref, f32[32,2304]{1,0:T(8,128)} %get-tuple-element.13.r_ref, f32[128,2304]{1,0:T(8,128)} %get-tuple-element.14.c_ref, f32[2,768]{1,0:T(2,128)} %bitcast.20, ...), custom_call_target="tpu_custom_call" | custom-call | flops 12884901888 | bytes 12582912 | tf_op jit(solution)/shard_map/attend/pallas_call | solution.py:689
  227.8 2.7 %copy.15 = bf16[128,6144]{1,0:T(8,128)(2,1)} copy(bf16[128,6144]{1,0:T(8,128)(2,1)} %attend.1) | data formatting | bytes 3145728
  (4 shorter events, 0.0 us)
Async XLA Ops:
  2.8 1.3 copy-start
  2.8 1.9 copy-start.1
